TPU v7x, 64 devices: a 2x2x8 block of a 4x4x8 slice. The times are simulated.
64 devices in a mesh: rep: 4 (over x, y), dp: 16 (over z, core).
Axes of the slice: x: 2, y: 2, z: 8, core: 2. Of those that a mesh axis runs over, the one named last changes fastest.
The devices are a block of a 4x4x8 slice.
Arguments:
- x: bfloat16 [64, 2048, 768], P(('rep', 'dp')), parts along dimension 0
- dy: bfloat16 [64, 2048, 768], P(('rep', 'dp')), parts along dimension 0
- w_gate: bfloat16 [2, 768, 2304], replicated
- w_up: bfloat16 [2, 768, 2304], replicated
- w_down: bfloat16 [2, 2304, 768], replicated
- m_w_gate: float32 [2, 768, 2304], replicated
- m_w_up: float32 [2, 768, 2304], replicated
- m_w_down: float32 [2, 2304, 768], replicated
- v_w_gate: float32 [2, 768, 2304], replicated
- v_w_up: float32 [2, 768, 2304], replicated
- v_w_down: float32 [2, 2304, 768], replicated
Outputs:
- output 1: bfloat16 [8, 768, 2304], P('rep'), parts along dimension 0
- output 2: bfloat16 [8, 768, 2304], P('rep'), parts along dimension 0
- output 3: bfloat16 [8, 2304, 768], P('rep'), parts along dimension 0
- output 4: float32 [8, 768, 2304], P('rep'), parts along dimension 0
- output 5: float32 [8, 768, 2304], P('rep'), parts along dimension 0
- output 6: float32 [8, 2304, 768], P('rep'), parts along dimension 0
- output 7: float32 [8, 768, 2304], P('rep'), parts along dimension 0
- output 8: float32 [8, 768, 2304], P('rep'), parts along dimension 0
- output 9: float32 [8, 2304, 768], P('rep'), parts along dimension 0
There are 4 independent parts. A program takes and returns all parts, laid end to end along the dimension named above; an argument that names none is the same for every part.
All inputs are finite; a program needn't handle non-finite values.
Results may differ from a plain program's by a relative error of at most 0.0224.
Values are sent between devices in bfloat16 or wider.
A program may use at most 768 MiB of HBM per device.

v0:
```python
import functools

import jax
import jax.numpy as jnp
from jax import lax
from jax.experimental import pallas as pl
from jax.experimental.pallas import tpu as pltpu
from jax.sharding import PartitionSpec as P

MESH = pl.DeviceIdType.MESH
F32, BF16 = jnp.float32, jnp.bfloat16
EVERY = pl.BlockSpec(memory_space=pl.ANY)
VMEM = pl.BlockSpec(memory_space=pltpu.VMEM)


def rounded(a, b, contract=((1,), (0,))):
    return lax.dot_general(a, b, (contract, ((), ())), preferred_element_type=F32).astype(BF16)


def wide_dot(a, b):
    return jnp.dot(a, b, preferred_element_type=F32)


def scale_of(wide):
    return lax.rsqrt(jnp.mean(wide * wide, -1, keepdims=True) + 1e-6)


def normed(h):
    wide = h.astype(F32)
    return (wide * scale_of(wide)).astype(BF16)


def gated(gate, up):
    return (gate * jax.nn.sigmoid(gate) * up).astype(BF16)


def gated_back(gate, up, by_mid):
    by_mid = by_mid.astype(F32)
    one = jax.nn.sigmoid(gate)
    silu = gate * one
    by_gate = by_mid * up * (one * (1.0 + gate * (1.0 - one)))
    return (silu * up).astype(BF16), by_gate.astype(BF16), (by_mid * silu).astype(BF16)


def params(mib, **more):
    return pltpu.CompilerParams(vmem_limit_bytes=mib << 20, **more)


def cost(matmuls, tokens, d, ff, moved):
    return pl.CostEstimate(flops=2 * matmuls * tokens * d * ff, bytes_accessed=moved, transcendentals=tokens * ff)


def up_kernel(h_ref, gate_ref, up_ref, a_ref, mid_ref):
    @pl.when(pl.program_id(1) == 0)
    def _():
        a_ref[...] = normed(h_ref[...])

    a = a_ref[...]
    mid_ref[...] = gated(wide_dot(a, gate_ref[0]), wide_dot(a, up_ref[0]))


def columns_of(number, d, block):
    return pl.BlockSpec((1, d, block), lambda i, k: (number, 0, k))


def rows_of(number, d, block):
    return pl.BlockSpec((1, block, d), lambda i, k: (number, k, 0))


def forward_up(number, h, w_gate, w_up, tall=1024, block=768):
    tokens, d = h.shape
    ff = w_gate.shape[2]
    rows = pl.BlockSpec((tall, d), lambda i, k: (i, 0))
    part = pl.BlockSpec((tall, block), lambda i, k: (i, k))
    return pl.pallas_call(
        up_kernel,
        out_shape=(jax.ShapeDtypeStruct((tokens, d), BF16), jax.ShapeDtypeStruct((tokens, ff), BF16)),
        grid=(tokens // tall, ff // block),
        in_specs=[rows, columns_of(number, d, block), columns_of(number, d, block)],
        out_specs=(rows, part),
        compiler_params=params(50),
        cost_estimate=cost(2, tokens, d, ff, 26 << 20),
        name="forward_up",
    )(h, w_gate, w_up)


def down_kernel(mid_ref, down_ref, h_ref, out_ref):
    out_ref[...] = h_ref[...] + rounded(mid_ref[...], down_ref[0])


def forward_down(number, mid, w_down, h, tall=512):
    tokens, d = h.shape
    ff = mid.shape[1]
    rows = pl.BlockSpec((tall, d), lambda i: (i, 0))
    return pl.pallas_call(
        down_kernel,
        out_shape=jax.ShapeDtypeStruct((tokens, d), BF16),
        grid=(tokens // tall,),
        in_specs=[pl.BlockSpec((tall, ff), lambda i: (i, 0)), pl.BlockSpec((1, ff, d), lambda i: (number, 0, 0)), rows],
        out_specs=rows,
        compiler_params=params(50),
        cost_estimate=cost(1, tokens, d, ff, 20 << 20),
        name="forward_down",
    )(mid, w_down, h)


def last_kernel(h_ref, by_ref, gate_ref, up_ref, down_ref, a_ref, mid_ref, by_gate_ref, by_up_ref):
    @pl.when(pl.program_id(1) == 0)
    def _():
        a_ref[...] = normed(h_ref[...])

    a = a_ref[...]
    by_mid = rounded(by_ref[...], down_ref[0], ((1,), (1,)))
    mid_ref[...], by_gate_ref[...], by_up_ref[...] = gated_back(wide_dot(a, gate_ref[0]), wide_dot(a, up_ref[0]), by_mid)


def last_layer(number, h, by, w_gate, w_up, w_down, tall=1024, block=768):
    tokens, d = h.shape
    ff = w_gate.shape[2]
    rows = pl.BlockSpec((tall, d), lambda i, k: (i, 0))
    part = pl.BlockSpec((tall, block), lambda i, k: (i, k))
    return pl.pallas_call(
        last_kernel,
        out_shape=(jax.ShapeDtypeStruct((tokens, d), BF16),) + (jax.ShapeDtypeStruct((tokens, ff), BF16),) * 3,
        grid=(tokens // tall, ff // block),
        in_specs=[rows, rows, columns_of(number, d, block), columns_of(number, d, block), rows_of(number, d, block)],
        out_specs=(rows, part, part, part),
        compiler_params=params(60),
        cost_estimate=cost(3, tokens, d, ff, 60 << 20),
        name="last_layer",
    )(h, by, w_gate, w_up, w_down)


def weight_kernel(a_ref, by_ref, mid_ref, by_gate_ref, by_up_ref, gate_ref, up_ref, down_ref, turned):
    @pl.when(pl.program_id(0) == 0)
    def _():
        turned[...] = a_ref[...].T

    gate_ref[...] = rounded(turned[...], by_gate_ref[...])
    up_ref[...] = rounded(turned[...], by_up_ref[...])
    down_ref[...] = rounded(mid_ref[...], by_ref[...], ((0,), (0,)))


def by_weights(a, by, mid, by_gate, by_up, block=768):
    tokens, d = a.shape
    ff = mid.shape[1]
    whole = pl.BlockSpec((tokens, d), lambda k: (0, 0), pipeline_mode=pl.Buffered(1))
    part = pl.BlockSpec((tokens, block), lambda k: (0, k))
    out = pl.BlockSpec((d, block), lambda k: (0, k))
    return pl.pallas_call(
        weight_kernel,
        out_shape=(jax.ShapeDtypeStruct((d, ff), BF16),) * 2 + (jax.ShapeDtypeStruct((ff, d), BF16),),
        grid=(ff // block,),
        in_specs=[whole, whole, part, part, part],
        out_specs=(out, out, pl.BlockSpec((block, d), lambda k: (k, 0))),
        scratch_shapes=[pltpu.VMEM((d, tokens), BF16)],
        compiler_params=params(56),
        cost_estimate=cost(3, tokens, d, ff, 45 << 20),
        name="by_weights",
    )(a, by, mid, by_gate, by_up)


class Ring:
    def __init__(self, n, grads, refs):
        self.n, self.chips, self.grads = n, n // 2, grads
        self.wide_own, self.wide_pair, self.wide_ring, self.tall_own, self.tall_pair, self.tall_ring = refs[:6]
        self.local, self.pair_send, self.pair_recv, self.ring_send, self.ring_recv = refs[6:]
        self.me = lax.axis_index("dp")
        self.z, self.c = self.me // 2, lax.rem(self.me, 2)
        self.partner = self.z * 2 + 1 - self.c
        self.beside = [lax.rem(self.z + k, self.chips) * 2 + self.c for k in (1, self.chips - 1)]

    @staticmethod
    def scratch(n, wide, tall):
        chips, sem = n // 2, pltpu.SemaphoreType.DMA
        return [
            pltpu.VMEM((2, chips, *wide), BF16),
            pltpu.VMEM((2, chips, *wide), BF16),
            pltpu.VMEM((2, chips - 1, *wide), BF16),
            pltpu.VMEM((chips, *tall), BF16),
            pltpu.VMEM((chips, *tall), BF16),
            pltpu.VMEM((chips - 1, *tall), BF16),
            sem((3, chips)), sem((3, chips)), sem((3, chips)), sem((3, 2, chips - 1)), sem((3, 2, chips - 1)),
        ]

    def chunk(self, way, step):
        return lax.rem(self.z + self.chips + ((-1 - step) if way == 0 else (1 + step - self.chips)), self.chips)

    def refs(self, i, j):
        if i < 2:
            return self.wide_own.at[i, j], self.wide_pair.at[i, j], lambda step: self.wide_ring.at[i, step]
        return self.tall_own.at[j], self.tall_pair.at[j], lambda step: self.tall_ring.at[step]

    def exchange(self, i, j):
        own, pair, _ = self.refs(i, j)
        return (
            pltpu.make_async_copy(self.grads[i].at[j, self.c], own, self.local.at[i, j]),
            pltpu.make_async_remote_copy(
                src_ref=self.grads[i].at[j, 1 - self.c], dst_ref=pair, send_sem=self.pair_send.at[i, j], recv_sem=self.pair_recv.at[i, j],
                device_id={"dp": self.partner}, device_id_type=MESH,
            ),
        )

    def greet(self, everyone):
        barrier = pltpu.get_barrier_semaphore()
        others = [lax.rem(self.me + k, self.n) for k in range(1, self.n)] if everyone else [self.partner, *self.beside]
        for other in others:
            pl.semaphore_signal(barrier, inc=1, device_id={"dp": other}, device_id_type=MESH)
        pl.semaphore_wait(barrier, len(others))

    def new_chunks(self, step):
        half = self.chips // 2
        if step < half - 1:
            return [self.chunk(0, step), self.chunk(1, step)]
        return [self.chunk(0, step)] if step in (half - 1, self.chips - 1) else []

    def begin(self):
        for step in range(self.chips):
            for j in self.new_chunks(step):
                for i in range(3):
                    for copy in self.exchange(i, j):
                        copy.start()

    def half(self, i, way):
        columns = self.grads[i].shape[3] // 2
        return slice(None), slice(columns * way, columns * (way + 1))

    def hop(self, i, way, step):
        own, _, ring = self.refs(i, self.chunk(way, step))
        at = self.half(i, way)
        return pltpu.make_async_remote_copy(
            src_ref=own.at[at], dst_ref=ring(step).at[at], send_sem=self.ring_send.at[i, way, step], recv_sem=self.ring_recv.at[i, way, step],
            device_id={"dp": self.beside[way]}, device_id_type=MESH,
        )

    def ready(self, i, step):
        for j in self.new_chunks(step):
            for copy in self.exchange(i, j):
                copy.wait()

    def total(self, i, j, at, step):
        own, pair, ring = self.refs(i, j)
        value = own[at].astype(F32) + pair[at].astype(F32)
        if step:
            value = value + ring(step - 1)[at].astype(F32)
        return value.astype(BF16)

    def send(self, step):
        for i in range(3):
            self.ready(i, step)
            for way in range(2):
                if step:
                    self.hop(i, way, step - 1).wait_recv()
                j, at = self.chunk(way, step), self.half(i, way)
                self.refs(i, j)[0][at] = self.total(i, j, at, step)
            for way in range(2):
                self.hop(i, way, step).start()

    def finish(self, out):
        last = self.chips - 1
        for i in range(3):
            self.ready(i, last)
            for way in range(2):
                self.hop(i, way, last - 1).wait_recv()
            value = self.total(i, self.z, (slice(None), slice(None)), last)
            rows, columns = out.shape[1], value.shape[1]
            for k in range(value.shape[0] // rows):
                out[i, :, columns * k : columns * (k + 1)] = value[rows * k : rows * (k + 1)]
        for i in range(3):
            for way in range(2):
                for step in range(last):
                    self.hop(i, way, step).wait_send()


def squares_of(ref):
    squares = jnp.zeros((8, 128), F32)
    for i in range(ref.shape[0]):
        value = ref[i].astype(F32)
        flat = jnp.sum((value * value).reshape(-1, 8, value.shape[1]), axis=0)
        for k in range(flat.shape[1] // 128):
            squares = squares + flat[:, 128 * k : 128 * (k + 1)]
    return squares


def ring_kernel(n, *refs):
    grads, before_ref, out_ref, ss_ref, parts, ss_send, ss_recv = refs[:3], *refs[3:9]
    ring = Ring(n, grads, refs[9:])
    ring.greet(True)
    ring.begin()
    for step in range(ring.chips - 1):
        ring.send(step)
    me = ring.me
    before = squares_of(before_ref)
    ring.finish(out_ref)
    parts[me] = before + squares_of(out_ref)

    def tell(k):
        return pltpu.make_async_remote_copy(
            src_ref=parts.at[me], dst_ref=parts.at[me], send_sem=ss_send.at[k], recv_sem=ss_recv.at[k],
            device_id={"dp": lax.rem(me + k, n)}, device_id_type=MESH,
        )

    for k in range(1, n):
        tell(k).start()
    for k in range(1, n):
        tell(k).wait()
    everyone = parts[0]
    for k in range(1, n):
        everyone = everyone + parts[k]
    ss_ref[...] = everyone


def chunked(n, grads):
    return [g.reshape(n // 2, 2, g.shape[0] // n, g.shape[1]) for g in grads]


def summed(n, grads, before):
    shaped = chunked(n, grads)
    wide, tall = shaped[0].shape[2:], shaped[2].shape[2:]
    return pl.pallas_call(
        functools.partial(ring_kernel, n),
        out_shape=(jax.ShapeDtypeStruct((3, *wide), BF16), jax.ShapeDtypeStruct((8, 128), F32)),
        in_specs=[EVERY] * 3 + [VMEM],
        out_specs=(VMEM,) * 2,
        scratch_shapes=[pltpu.VMEM((n, 8, 128), F32), pltpu.SemaphoreType.DMA((n,)), pltpu.SemaphoreType.DMA((n,)), *Ring.scratch(n, wide, tall)],
        compiler_params=params(40, collective_id=0, has_side_effects=True),
        name="ring_sum",
    )(*shaped, before)


def first_kernel(n, block, *refs):
    grads = refs[:3]
    by_gate1, by_up1, gate1, up1, h1, by1, gate0, up0, down0, a0 = refs[3:13]
    out_ref, by_ref, by_gate_ref, by_up_ref = refs[13:17]
    ring = Ring(n, grads, refs[17:])
    tile = pl.program_id(0)
    tiles = (ring.chips - 1 + 1) // 2

    @pl.when(tile == 0)
    def _():
        ring.greet(False)
        ring.begin()

    def moment(which):
        for k in range(tiles):
            step = 2 * k + which

            @pl.when(tile == k)
            def _():
                if step < ring.chips - 1:
                    ring.send(step)
                else:
                    ring.finish(out_ref)

    last = ((1,), (1,))
    by_a = rounded(by_gate1[...], gate1[0], last) + rounded(by_up1[...], up1[0], last)
    wide, by_a = h1[...].astype(F32), by_a.astype(F32)
    scale = scale_of(wide)
    dots = jnp.sum(by_a * wide, -1, keepdims=True) / wide.shape[1]
    by_ref[...] = by1[...] + (by_a * scale - wide * (scale * scale * scale * dots)).astype(BF16)
    moment(0)
    by, a = by_ref[...], a0[...]
    for k in range(gate0.shape[2] // block):
        at = slice(block * k, block * (k + 1))
        by_mid = rounded(by, down0[0, at, :], last)
        _, by_gate_ref[:, at], by_up_ref[:, at] = gated_back(wide_dot(a, gate0[0, :, at]), wide_dot(a, up0[0, :, at]), by_mid)
    moment(1)


def first_layer(n, grads, by_gate, by_up, h, by, a, w_gate, w_up, w_down, block=768):
    shaped = chunked(n, grads)
    wide, tall = shaped[0].shape[2:], shaped[2].shape[2:]
    tokens, d = h.shape
    ff = by_gate.shape[1]
    deep = tokens // (n // 4)

    def whole(number, w):
        return pl.BlockSpec((1, *w.shape[1:]), lambda i: (number, 0, 0), pipeline_mode=pl.Buffered(1))

    rows, long = pl.BlockSpec((deep, d), lambda i: (i, 0)), pl.BlockSpec((deep, ff), lambda i: (i, 0))
    return pl.pallas_call(
        functools.partial(first_kernel, n, block),
        out_shape=(
            jax.ShapeDtypeStruct((3, *wide), BF16),
            jax.ShapeDtypeStruct((tokens, d), BF16),
            jax.ShapeDtypeStruct((tokens, ff), BF16),
            jax.ShapeDtypeStruct((tokens, ff), BF16),
        ),
        grid=(n // 4,),
        in_specs=[EVERY] * 3 + [long, long, whole(1, w_gate), whole(1, w_up), rows, rows, whole(0, w_gate), whole(0, w_up), whole(0, w_down), rows],
        out_specs=(pl.BlockSpec((3, *wide), lambda i: (0, 0, 0)), rows, long, long),
        scratch_shapes=Ring.scratch(n, wide, tall),
        compiler_params=params(60, collective_id=1, has_side_effects=True, dimension_semantics=("arbitrary",)),
        cost_estimate=cost(5, tokens, d, ff, 60 << 20),
        name="first_layer",
    )(*shaped, by_gate, by_up, w_gate, w_up, h, by, w_gate, w_up, w_down, a)


def adam_kernel(first, where_ref, factor_ref, *refs):
    pieces, (w, m, v) = refs[:4], (refs[4:7], refs[7:10], refs[10:13])
    new_w, new_m, new_v = (refs[i : i + 3] for i in ((13, 16, 19) if first else (22, 25, 28)))
    g_ref = refs[-1]
    part = pl.program_id(0)
    for p in range(4):

        @pl.when(part == p)
        def _():
            g_ref[...] = pieces[p][...]

    factor = factor_ref[0]
    for which in range(3):
        rows, columns = w[which].shape[1:]
        deep = g_ref.shape[1]
        for k in range(rows // deep):
            at = (0, slice(deep * k, deep * (k + 1)), slice(None))
            g = g_ref[which, :, columns * k : columns * (k + 1)].astype(F32) * factor
            mean = 0.9 * m[which][at] + 0.1 * g
            square = 0.95 * v[which][at] + 0.05 * g * g
            wide = w[which][at].astype(F32)
            new_m[which][at] = mean
            new_v[which][at] = square
            new_w[which][at] = (wide - 0.02 * (mean * lax.rsqrt(square + 1e-8) + 0.1 * wide)).astype(BF16)


def adam(n, where, factor, pieces, state, so_far):
    first = so_far is None
    shapes = [jax.ShapeDtypeStruct(s.shape, s.dtype) for s in state]

    def block(s):
        return pl.BlockSpec((1, s.shape[1] // n, s.shape[2]), lambda p, where, factor: (where[0, p], where[1, p], 0))

    whole = pl.BlockSpec(pieces[0].shape, lambda p, where, factor: (0, 0, 0))
    size = sum(s.size // n for s in state[:3]) * 4
    return pl.pallas_call(
        functools.partial(adam_kernel, first),
        out_shape=shapes,
        grid_spec=pltpu.PrefetchScalarGridSpec(
            num_scalar_prefetch=2,
            grid=(4,),
            in_specs=[whole] * 4 + [block(s) for s in state] + ([] if first else [EVERY] * 9),
            out_specs=[block(s) for s in state],
            scratch_shapes=[pltpu.VMEM(pieces[0].shape, BF16)],
        ),
        input_output_aliases={} if first else {15 + i: i for i in range(9)},
        compiler_params=pltpu.CompilerParams(vmem_limit_bytes=40 << 20, dimension_semantics=("arbitrary",)),
        cost_estimate=pl.CostEstimate(flops=60_000_000, bytes_accessed=size * 11, transcendentals=size // 4),
        name="adam_step",
    )(where, factor, *pieces, *state, *(so_far or ()))


def solution(mesh):
    n = mesh.shape["dp"]
    chips = n // 2

    def step(x, dy, *arrays):
        weights, m, v = (arrays[i : i + 3] for i in (0, 3, 6))
        w_gate, w_up, w_down = weights
        x, dy = x[0], dy[0]
        a0, mid0 = forward_up(0, x, w_gate, w_up)
        h1 = forward_down(0, mid0, w_down, x)
        a1, mid1, by_gate1, by_up1 = last_layer(1, h1, dy, w_gate, w_up, w_down)
        grads1 = by_weights(a1, dy, mid1, by_gate1, by_up1)
        right, by, by_gate0, by_up0 = first_layer(n, grads1, by_gate1, by_up1, h1, dy, a0, w_gate, w_up, w_down)
        grads0 = by_weights(a0, by, mid0, by_gate0, by_up0)
        left, squares = summed(n, grads0, right)
        count = sum(w.size for w in weights)
        factor = jnp.minimum(1.0, 0.5 * lax.rsqrt(jnp.sum(squares) / count + 1e-30)).reshape(1)

        me = lax.axis_index("dp")
        z, c = me // 2, me % 2
        ahead = [(i, (i + 2) % n) for i in range(n)]
        behind = [(i, (i + n - 2) % n) for i in range(n)]
        pairs = [(i, i ^ 1) for i in range(n)]
        new = None
        for hop in range(chips):
            if hop:
                right = lax.ppermute(right, "dp", ahead)
                left = lax.ppermute(left, "dp", behind)
            pieces = [right, lax.ppermute(right, "dp", pairs), left, lax.ppermute(left, "dp", pairs)]
            from_right, from_left = (z + chips - hop) % chips * 2, (z + hop) % chips * 2
            where = jnp.array([[1, 1, 0, 0], [0, 0, 0, 0]], jnp.int32).at[1].set(
                jnp.stack([from_right + c, from_right + 1 - c, from_left + c, from_left + 1 - c])
            )
            new = adam(n, where, factor, pieces, (*weights, *m, *v), new)
        return tuple(new)

    return jax.shard_map(
        step,
        mesh=mesh,
        in_specs=(P(("rep", "dp"), None, None),) * 2 + (P(None, None, None),) * 9,
        out_specs=(P("rep", None, None),) * 9,
        check_vma=False,
    )
```

profile of v0, /device:TPU:21, one launch (start us, length us, event | category | flops | bytes accessed | tf_op | source)
XLA Modules:
  0.0 500.1 jit_solution(16711542047118328623)
XLA Ops:
  0.6 20.2 %forward_up.1 = (bf16[2048,768]{1,0:T(8,128)(2,1)S(1)}, bf16[2048,2304]{1,0:T(8,128)(2,1)}) custom-call(bf16[2048,768]{1,0:T(8,128)(2,1)} %bitcast.46, bf16[2,768,2304]{2,1,0:T(8,128)(2,1)} %refs_4_.15, bf16[2,768,2304]{2,1,0:T(8,128)(2,1)} %refs_5_.17), custom_call_target="tpu_custom_call" | custom-call | flops 14495514624 | bytes 27262976 | tf_op jit(solution)/shard_map/forward_up/pallas_call | solution.py:75
  22.5 11.0 %forward_down.1.h_ref.refs_7_ = bf16[2048,768]{1,0:T(8,128)(2,1)S(1)} custom-call(bf16[2048,2304]{1,0:T(8,128)(2,1)} %get-tuple-element.187.mid_ref, bf16[2,2304,768]{2,1,0:T(8,128)(2,1)} %refs_6_.17, bf16[2048,768]{1,0:T(8,128)(2,1)} %bitcast.47), custom_call_target="tpu_custom_call" | custom-call | flops 7247757312 | bytes 20971520 | tf_op jit(solution)/shard_map/forward_down/pallas_call | solution.py:95
  35.2 31.6 %last_layer.1 = (bf16[2048,768]{1,0:T(8,128)(2,1)}, bf16[2048,2304]{1,0:T(8,128)(2,1)}, bf16[2048,2304]{1,0:T(8,128)(2,1)}, bf16[2048,2304]{1,0:T(8,128)(2,1)}) custom-call(bf16[2048,768]{1,0:T(8,128)(2,1)} %copy-done.33, bf16[2048,768]{1,0:T(8,128)(2,1)} %bitcast.48, bf16[2,768,2304]{2,1,0:T(8,128)(2,1)} %refs_4_.15, bf16[2,768,2304]{2,1,0:T(8,128)(2,1)} %refs_5_.17, ...), custom_call_target="tpu_custom_call" | custom-call | flops 21743271936 | bytes 62914560 | tf_op jit(solution)/shard_map/last_layer/pallas_call | solution.py:122
  66.8 31.1 %by_weights.2 = (bf16[768,2304]{1,0:T(8,128)(2,1)}, bf16[768,2304]{1,0:T(8,128)(2,1)}, bf16[2304,768]{1,0:T(8,128)(2,1)}) custom-call(bf16[2048,768]{1,0:T(8,128)(2,1)} %get-tuple-element.188.a_ref, bf16[2048,768]{1,0:T(8,128)(2,1)} %bitcast.49, bf16[2048,2304]{1,0:T(8,128)(2,1)} %get-tuple-element.189.mid_ref, ...), custom_call_target="tpu_custom_call" | custom-call | flops 21743271936 | bytes 47185920 | tf_op jit(solution)/shard_map/by_weights/pallas_call | solution.py:150
  97.9 77.6 %first_layer.1 = (bf16[3,48,2304]{2,1,0:T(8,128)(2,1)}, bf16[2048,768]{1,0:T(8,128)(2,1)}, bf16[2048,2304]{1,0:T(8,128)(2,1)}, bf16[2048,2304]{1,0:T(8,128)(2,1)}) custom-call(bf16[8,2,48,2304]{3,2,1,0:T(8,128)(2,1)} %bitcast.51, bf16[8,2,48,2304]{3,2,1,0:T(8,128)(2,1)} %bitcast.52, bf16[8,2,144,768]{3,2,1,0:T(8,128)(2,1)} %bitcast.53, ...), custom_call_target="tpu_custom_call" | custom-call | flops 36238786560 | bytes 62914560 | tf_op jit(solution)/shard_map/first_layer/pallas_call | solution.py:381
  175.5 31.1 %by_weights.3 = (bf16[768,2304]{1,0:T(8,128)(2,1)}, bf16[768,2304]{1,0:T(8,128)(2,1)}, bf16[2304,768]{1,0:T(8,128)(2,1)}) custom-call(bf16[2048,768]{1,0:T(8,128)(2,1)} %copy-done.34, bf16[2048,768]{1,0:T(8,128)(2,1)} %get-tuple-element.195.by_ref, bf16[2048,2304]{1,0:T(8,128)(2,1)} %get-tuple-element.187.mid_ref, ...), custom_call_target="tpu_custom_call" | custom-call | flops 21743271936 | bytes 47185920 | tf_op jit(solution)/shard_map/by_weights/pallas_call | solution.py:150
  212.7 75.9 %ring_sum.1 = (bf16[3,48,2304]{2,1,0:T(8,128)(2,1)S(1)}, f32[8,128]{1,0:T(8,128)S(1)}) custom-call(bf16[8,2,48,2304]{3,2,1,0:T(8,128)(2,1)S(1)} %bitcast.43, bf16[8,2,48,2304]{3,2,1,0:T(8,128)(2,1)S(1)} %bitcast.44, bf16[8,2,144,768]{3,2,1,0:T(8,128)(2,1)S(1)} %bitcast.45, bf16[3,48,2304]{2,1,0:T(8,128)(2,1)S(1)} %copy-done.4), custom_call_target="tpu_custom_call" | custom-call | tf_op jit(solution)/shard_map/ring_sum/pallas_call | solution.py:320
  290.1 14.6 %collective-permute-done.8.refs_2_ = bf16[3,48,2304]{2,1,0:T(8,128)(2,1)S(1)} collective-permute-done((bf16[3,48,2304]{2,1,0:T(8,128)(2,1)S(1)}, bf16[3,48,2304]{2,1,0:T(8,128)(2,1)S(1)}, u32[]{:S(2)}, u32[]{:S(2)}) %collective-permute-start.8) | collective-permute-done | bytes 663584 | tf_op jit(solution)/shard_map/ppermute | solution.py:478
  306.3 13.6 %collective-permute-done.9.refs_2_ = bf16[3,48,2304]{2,1,0:T(8,128)(2,1)S(1)} collective-permute-done((bf16[3,48,2304]{2,1,0:T(8,128)(2,1)S(1)}, bf16[3,48,2304]{2,1,0:T(8,128)(2,1)S(1)}, u32[]{:S(2)}, u32[]{:S(2)}) %collective-permute-start.9) | collective-permute-done | bytes 663584 | tf_op jit(solution)/shard_map/ppermute | solution.py:478
  319.9 3.0 collective-permute-start.10
  323.0 2.4 collective-permute-start.29
  326.2 8.9 %collective-permute-done.10.refs_2_ = bf16[3,48,2304]{2,1,0:T(8,128)(2,1)S(1)} collective-permute-done((bf16[3,48,2304]{2,1,0:T(8,128)(2,1)S(1)}, bf16[3,48,2304]{2,1,0:T(8,128)(2,1)S(1)}, u32[]{:S(2)}, u32[]{:S(2)}) %collective-permute-start.10) | collective-permute-done | bytes 663584 | tf_op jit(solution)/shard_map/ppermute | solution.py:478
  335.1 3.4 collective-permute-start.11
  338.5 3.2 collective-permute-start.27
  345.6 4.2 collective-permute-done.11.refs_2_
  349.8 3.4 collective-permute-start.12
  354.2 4.1 collective-permute-start.24
  363.7 3.4 collective-permute-start.13
  368.0 5.3 %collective-permute-start.21 = (bf16[3,48,2304]{2,1,0:T(8,128)(2,1)S(1)}, bf16[3,48,2304]{2,1,0:T(8,128)(2,1)}, u32[]{:S(2)}, u32[]{:S(2)}) collective-permute-start(bf16[3,48,2304]{2,1,0:T(8,128)(2,1)S(1)} %collective-permute-done.11.refs_2_), channel_id=1, source_target_pairs={{0,1},{1,0},{2,3},{3,2},{4,5},{5,4},{6,7},{7,6},{8,9},{9,8},{10,11... | collective-permute-start | bytes 1990664 | tf_op jit(solution)/shard_map/ppermute | solution.py:479
  377.0 3.5 collective-permute-start.14
  382.3 6.8 %collective-permute-start.18 = (bf16[3,48,2304]{2,1,0:T(8,128)(2,1)}, bf16[3,48,2304]{2,1,0:T(8,128)(2,1)}, u32[]{:S(2)}, u32[]{:S(2)}) collective-permute-start(bf16[3,48,2304]{2,1,0:T(8,128)(2,1)} %collective-permute-done.4.refs_0_), channel_id=1, source_target_pairs={{0,1},{1,0},{2,3},{3,2},{4,5},{5,4},{6,7},{7,6},{8,9},{9,8},{10,11... | collective-permute-start | bytes 1990664 | tf_op jit(solution)/shard_map/ppermute | solution.py:479
  390.5 6.4 %collective-permute-start.15 = (bf16[3,48,2304]{2,1,0:T(8,128)(2,1)}, bf16[3,48,2304]{2,1,0:T(8,128)(2,1)}, u32[]{:S(2)}, u32[]{:S(2)}) collective-permute-start(bf16[3,48,2304]{2,1,0:T(8,128)(2,1)} %collective-permute-done.14.refs_2_), channel_id=1, source_target_pairs={{0,1},{1,0},{2,3},{3,2},{4,5},{5,4},{6,7},{7,6},{8,9},{9,8},{10,11... | collective-permute-start | bytes 1990664 | tf_op jit(solution)/shard_map/ppermute | solution.py:479
  396.9 3.4 collective-permute-start.7
  401.0 3.0 copy-done
  407.3 11.2 %adam_step.8 = (bf16[2,768,2304]{2,1,0:T(8,128)(2,1)}, bf16[2,768,2304]{2,1,0:T(8,128)(2,1)}, bf16[2,2304,768]{2,1,0:T(8,128)(2,1)}, f32[2,768,2304]{2,1,0:T(8,1...) custom-call(s32[2,4]{1,0:T(2,128)S(1)} %scatter.39.where_ref, ...), custom_call_target="tpu_custom_call" | custom-call | flops 60000000 | bytes 29196288 | tf_op jit(solution)/shard_map/adam_step/pallas_call | solution.py:434
  418.5 11.2 %adam_step.9 = (bf16[2,768,2304]{2,1,0:T(8,128)(2,1)}, bf16[2,768,2304]{2,1,0:T(8,128)(2,1)}, bf16[2,2304,768]{2,1,0:T(8,128)(2,1)}, f32[2,768,2304]{2,1,0:T(8,1...) custom-call(s32[2,4]{1,0:T(2,128)S(1)} %scatter.36.where_ref, ...), custom_call_target="tpu_custom_call", output_to_operand_aliasing={{0}: (15, {}), {1}: (16, {}), {2}: (17, {}), {3}: (18, {}),... | custom-call | flops 60000000 | bytes 29196288 | tf_op jit(solution)/shard_map/adam_step/pallas_call | solution.py:434
  429.8 11.2 %adam_step.10 = (bf16[2,768,2304]{2,1,0:T(8,128)(2,1)}, bf16[2,768,2304]{2,1,0:T(8,128)(2,1)}, bf16[2,2304,768]{2,1,0:T(8,128)(2,1)}, f32[2,768,2304]{2,1,0:T(8,...) custom-call(s32[2,4]{1,0:T(2,128)S(1)} %scatter.35.where_ref, ...), custom_call_target="tpu_custom_call", output_to_operand_aliasing={{0}: (15, {}), {1}: (16, {}), {2}: (17, {}), {3}: (18, {}),... | custom-call | flops 60000000 | bytes 29196288 | tf_op jit(solution)/shard_map/adam_step/pallas_call | solution.py:434
  441.0 11.2 %adam_step.11 = (bf16[2,768,2304]{2,1,0:T(8,128)(2,1)}, bf16[2,768,2304]{2,1,0:T(8,128)(2,1)}, bf16[2,2304,768]{2,1,0:T(8,128)(2,1)}, f32[2,768,2304]{2,1,0:T(8,...) custom-call(s32[2,4]{1,0:T(2,128)S(1)} %scatter.34.where_ref, ...), custom_call_target="tpu_custom_call", output_to_operand_aliasing={{0}: (15, {}), {1}: (16, {}), {2}: (17, {}), {3}: (18, {}),... | custom-call | flops 60000000 | bytes 29196288 | tf_op jit(solution)/shard_map/adam_step/pallas_call | solution.py:434
  452.2 11.6 %adam_step.12 = (bf16[2,768,2304]{2,1,0:T(8,128)(2,1)}, bf16[2,768,2304]{2,1,0:T(8,128)(2,1)}, bf16[2,2304,768]{2,1,0:T(8,128)(2,1)}, f32[2,768,2304]{2,1,0:T(8,...) custom-call(s32[2,4]{1,0:T(2,128)S(1)} %scatter.31.where_ref, ...), custom_call_target="tpu_custom_call", output_to_operand_aliasing={{0}: (15, {}), {1}: (16, {}), {2}: (17, {}), {3}: (18, {}),... | custom-call | flops 60000000 | bytes 29196288 | tf_op jit(solution)/shard_map/adam_step/pallas_call | solution.py:434
  463.8 11.7 %adam_step.13 = (bf16[2,768,2304]{2,1,0:T(8,128)(2,1)}, bf16[2,768,2304]{2,1,0:T(8,128)(2,1)}, bf16[2,2304,768]{2,1,0:T(8,128)(2,1)}, f32[2,768,2304]{2,1,0:T(8,...) custom-call(s32[2,4]{1,0:T(2,128)S(1)} %scatter.30.where_ref, ...), custom_call_target="tpu_custom_call", output_to_operand_aliasing={{0}: (15, {}), {1}: (16, {}), {2}: (17, {}), {3}: (18, {}),... | custom-call | flops 60000000 | bytes 29196288 | tf_op jit(solution)/shard_map/adam_step/pallas_call | solution.py:434
  475.5 12.1 %adam_step.14 = (bf16[2,768,2304]{2,1,0:T(8,128)(2,1)}, bf16[2,768,2304]{2,1,0:T(8,128)(2,1)}, bf16[2,2304,768]{2,1,0:T(8,128)(2,1)}, f32[2,768,2304]{2,1,0:T(8,...) custom-call(s32[2,4]{1,0:T(2,128)S(1)} %scatter.29.where_ref, ...), custom_call_target="tpu_custom_call", output_to_operand_aliasing={{0}: (15, {}), {1}: (16, {}), {2}: (17, {}), {3}: (18, {}),... | custom-call | flops 60000000 | bytes 29196288 | tf_op jit(solution)/shard_map/adam_step/pallas_call | solution.py:434
  487.6 12.1 %adam_step.15 = (bf16[2,768,2304]{2,1,0:T(8,128)(2,1)}, bf16[2,768,2304]{2,1,0:T(8,128)(2,1)}, bf16[2,2304,768]{2,1,0:T(8,128)(2,1)}, f32[2,768,2304]{2,1,0:T(8,...) custom-call(s32[2,4]{1,0:T(2,128)S(1)} %scatter.26.where_ref, ...), custom_call_target="tpu_custom_call", output_to_operand_aliasing={{0}: (15, {}), {1}: (16, {}), {2}: (17, {}), {3}: (18, {}),... | custom-call | flops 60000000 | bytes 29196288 | tf_op jit(solution)/shard_map/adam_step/pallas_call | solution.py:434
  (140 shorter events, 34.4 us)
Async XLA Ops:
  175.5 31.1 %copy-start.4 = (bf16[3,48,2304]{2,1,0:T(8,128)(2,1)S(1)}, bf16[3,48,2304]{2,1,0:T(8,128)(2,1)}, u32[]{:S(2)}) copy-start(bf16[3,48,2304]{2,1,0:T(8,128)(2,1)} %get-tuple-element.201.refs_3_.refs_0_) | copy-start | bytes 1990660
  175.5 205.0 %copy-start.35 = (s32[2,4]{1,0:T(2,128)S(1)}, s32[2,4]{1,0:T(2,128)}, u32[]{:S(2)}) copy-start(s32[2,4]{1,0:T(2,128)} %constant.302.clone) | copy-start | bytes 100
  288.5 16.2 %collective-permute-start.8 = (bf16[3,48,2304]{2,1,0:T(8,128)(2,1)S(1)}, bf16[3,48,2304]{2,1,0:T(8,128)(2,1)S(1)}, u32[]{:S(2)}, u32[]{:S(2)}) collective-permute-start(bf16[3,48,2304]{2,1,0:T(8,128)(2,1)S(1)} %get-tuple-element.203.refs_2_), channel_id=1, source_target_pairs={{0,14},{1,15},{2,0},{3,1},{4,2},{5,3},{6,4},{7,5},{8,6},{9,7},{10,... | collective-permute-start | bytes 1990664 | tf_op jit(solution)/shard_map/ppermute | solution.py:478
  289.0 17.3 %collective-permute-start = (bf16[3,48,2304]{2,1,0:T(8,128)(2,1)S(1)}, bf16[3,48,2304]{2,1,0:T(8,128)(2,1)S(1)}, u32[]{:S(2)}, u32[]{:S(2)}) collective-permute-start(bf16[3,48,2304]{2,1,0:T(8,128)(2,1)S(1)} %copy-done.4), channel_id=1, source_target_pairs={{0,2},{1,3},{2,4},{3,5},{4,6},{5,7},{6,8},{7,9},{8,10},{9,11},{10,... | collective-permute-start | bytes 1990664 | tf_op jit(solution)/shard_map/ppermute | solution.py:477
  304.7 15.2 %collective-permute-start.9 = (bf16[3,48,2304]{2,1,0:T(8,128)(2,1)S(1)}, bf16[3,48,2304]{2,1,0:T(8,128)(2,1)S(1)}, u32[]{:S(2)}, u32[]{:S(2)}) collective-permute-start(bf16[3,48,2304]{2,1,0:T(8,128)(2,1)S(1)} %collective-permute-done.8.refs_2_), channel_id=1, source_target_pairs={{0,14},{1,15},{2,0},{3,1},{4,2},{5,3},{6,4},{7,5},{8,6},{9,7},{10,... | collective-permute-start | bytes 1990664 | tf_op jit(solution)/shard_map/ppermute | solution.py:478
  306.3 16.6 %collective-permute-start.1 = (bf16[3,48,2304]{2,1,0:T(8,128)(2,1)S(1)}, bf16[3,48,2304]{2,1,0:T(8,128)(2,1)S(1)}, u32[]{:S(2)}, u32[]{:S(2)}) collective-permute-start(bf16[3,48,2304]{2,1,0:T(8,128)(2,1)S(1)} %collective-permute-done.refs_0_), channel_id=1, source_target_pairs={{0,2},{1,3},{2,4},{3,5},{4,6},{5,7},{6,8},{7,9},{8,10},{9,11},{10,... | collective-permute-start | bytes 1990664 | tf_op jit(solution)/shard_map/ppermute | solution.py:477
  319.9 15.2 %collective-permute-start.10 = (bf16[3,48,2304]{2,1,0:T(8,128)(2,1)S(1)}, bf16[3,48,2304]{2,1,0:T(8,128)(2,1)S(1)}, u32[]{:S(2)}, u32[]{:S(2)}) collective-permute-start(bf16[3,48,2304]{2,1,0:T(8,128)(2,1)S(1)} %collective-permute-done.9.refs_2_), channel_id=1, source_target_pairs={{0,14},{1,15},{2,0},{3,1},{4,2},{5,3},{6,4},{7,5},{8,6},{9,7},{10,... | collective-permute-start | bytes 1990664 | tf_op jit(solution)/shard_map/ppermute | solution.py:478
  323.0 15.6 %collective-permute-start.2 = (bf16[3,48,2304]{2,1,0:T(8,128)(2,1)S(1)}, bf16[3,48,2304]{2,1,0:T(8,128)(2,1)S(1)}, u32[]{:S(2)}, u32[]{:S(2)}) collective-permute-start(bf16[3,48,2304]{2,1,0:T(8,128)(2,1)S(1)} %collective-permute-done.1.refs_0_), channel_id=1, source_target_pairs={{0,2},{1,3},{2,4},{3,5},{4,6},{5,7},{6,8},{7,9},{8,10},{9,11},{10,... | collective-permute-start | bytes 1990664 | tf_op jit(solution)/shard_map/ppermute | solution.py:477
  323.0 19.6 %collective-permute-start.29 = (bf16[3,48,2304]{2,1,0:T(8,128)(2,1)S(1)}, bf16[3,48,2304]{2,1,0:T(8,128)(2,1)S(1)}, u32[]{:S(2)}, u32[]{:S(2)}) collective-permute-start(bf16[3,48,2304]{2,1,0:T(8,128)(2,1)S(1)} %get-tuple-element.203.refs_2_), channel_id=1, source_target_pairs={{0,1},{1,0},{2,3},{3,2},{4,5},{5,4},{6,7},{7,6},{8,9},{9,8},{10,11... | collective-permute-start | bytes 1990664 | tf_op jit(solution)/shard_map/ppermute | solution.py:479
  326.2 18.1 %collective-permute-start.28 = (bf16[3,48,2304]{2,1,0:T(8,128)(2,1)S(1)}, bf16[3,48,2304]{2,1,0:T(8,128)(2,1)S(1)}, u32[]{:S(2)}, u32[]{:S(2)}) collective-permute-start(bf16[3,48,2304]{2,1,0:T(8,128)(2,1)S(1)} %copy-done.4), channel_id=1, source_target_pairs={{0,1},{1,0},{2,3},{3,2},{4,5},{5,4},{6,7},{7,6},{8,9},{9,8},{10,11... | collective-permute-start | bytes 1990664 | tf_op jit(solution)/shard_map/ppermute | solution.py:479
  335.1 14.7 %collective-permute-start.11 = (bf16[3,48,2304]{2,1,0:T(8,128)(2,1)S(1)}, bf16[3,48,2304]{2,1,0:T(8,128)(2,1)S(1)}, u32[]{:S(2)}, u32[]{:S(2)}) collective-permute-start(bf16[3,48,2304]{2,1,0:T(8,128)(2,1)S(1)} %collective-permute-done.10.refs_2_), channel_id=1, source_target_pairs={{0,14},{1,15},{2,0},{3,1},{4,2},{5,3},{6,4},{7,5},{8,6},{9,7},{10,... | collective-permute-start | bytes 1990664 | tf_op jit(solution)/shard_map/ppermute | solution.py:478
  338.5 14.7 %collective-permute-start.3 = (bf16[3,48,2304]{2,1,0:T(8,128)(2,1)S(1)}, bf16[3,48,2304]{2,1,0:T(8,128)(2,1)S(1)}, u32[]{:S(2)}, u32[]{:S(2)}) collective-permute-start(bf16[3,48,2304]{2,1,0:T(8,128)(2,1)S(1)} %collective-permute-done.2.refs_0_), channel_id=1, source_target_pairs={{0,2},{1,3},{2,4},{3,5},{4,6},{5,7},{6,8},{7,9},{8,10},{9,11},{10,... | collective-permute-start | bytes 1990664 | tf_op jit(solution)/shard_map/ppermute | solution.py:477
  338.5 14.7 %collective-permute-start.27 = (bf16[3,48,2304]{2,1,0:T(8,128)(2,1)S(1)}, bf16[3,48,2304]{2,1,0:T(8,128)(2,1)S(1)}, u32[]{:S(2)}, u32[]{:S(2)}) collective-permute-start(bf16[3,48,2304]{2,1,0:T(8,128)(2,1)S(1)} %collective-permute-done.8.refs_2_), channel_id=1, source_target_pairs={{0,1},{1,0},{2,3},{3,2},{4,5},{5,4},{6,7},{7,6},{8,9},{9,8},{10,11... | collective-permute-start | bytes 1990664 | tf_op jit(solution)/shard_map/ppermute | solution.py:479
  343.4 15.7 %collective-permute-start.26 = (bf16[3,48,2304]{2,1,0:T(8,128)(2,1)S(1)}, bf16[3,48,2304]{2,1,0:T(8,128)(2,1)S(1)}, u32[]{:S(2)}, u32[]{:S(2)}) collective-permute-start(bf16[3,48,2304]{2,1,0:T(8,128)(2,1)S(1)} %collective-permute-done.refs_0_), channel_id=1, source_target_pairs={{0,1},{1,0},{2,3},{3,2},{4,5},{5,4},{6,7},{7,6},{8,9},{9,8},{10,11... | collective-permute-start | bytes 1990664 | tf_op jit(solution)/shard_map/ppermute | solution.py:479
  345.2 15.7 %collective-permute-start.25 = (bf16[3,48,2304]{2,1,0:T(8,128)(2,1)S(1)}, bf16[3,48,2304]{2,1,0:T(8,128)(2,1)S(1)}, u32[]{:S(2)}, u32[]{:S(2)}) collective-permute-start(bf16[3,48,2304]{2,1,0:T(8,128)(2,1)S(1)} %collective-permute-done.9.refs_2_), channel_id=1, source_target_pairs={{0,1},{1,0},{2,3},{3,2},{4,5},{5,4},{6,7},{7,6},{8,9},{9,8},{10,11... | collective-permute-start | bytes 1990664 | tf_op jit(solution)/shard_map/ppermute | solution.py:479
  349.8 13.9 %collective-permute-start.12 = (bf16[3,48,2304]{2,1,0:T(8,128)(2,1)S(1)}, bf16[3,48,2304]{2,1,0:T(8,128)(2,1)S(1)}, u32[]{:S(2)}, u32[]{:S(2)}) collective-permute-start(bf16[3,48,2304]{2,1,0:T(8,128)(2,1)S(1)} %collective-permute-done.11.refs_2_), channel_id=1, source_target_pairs={{0,14},{1,15},{2,0},{3,1},{4,2},{5,3},{6,4},{7,5},{8,6},{9,7},{10,... | collective-permute-start | bytes 1990664 | tf_op jit(solution)/shard_map/ppermute | solution.py:478
  353.2 13.9 %collective-permute-start.4 = (bf16[3,48,2304]{2,1,0:T(8,128)(2,1)S(1)}, bf16[3,48,2304]{2,1,0:T(8,128)(2,1)}, u32[]{:S(2)}, u32[]{:S(2)}) collective-permute-start(bf16[3,48,2304]{2,1,0:T(8,128)(2,1)S(1)} %collective-permute-done.3.refs_0_), channel_id=1, source_target_pairs={{0,2},{1,3},{2,4},{3,5},{4,6},{5,7},{6,8},{7,9},{8,10},{9,11},{10,... | collective-permute-start | bytes 1990664 | tf_op jit(solution)/shard_map/ppermute | solution.py:477
  354.2 12.9 %collective-permute-start.24 = (bf16[3,48,2304]{2,1,0:T(8,128)(2,1)S(1)}, bf16[3,48,2304]{2,1,0:T(8,128)(2,1)S(1)}, u32[]{:S(2)}, u32[]{:S(2)}) collective-permute-start(bf16[3,48,2304]{2,1,0:T(8,128)(2,1)S(1)} %collective-permute-done.1.refs_0_), channel_id=1, source_target_pairs={{0,1},{1,0},{2,3},{3,2},{4,5},{5,4},{6,7},{7,6},{8,9},{9,8},{10,11... | collective-permute-start | bytes 1990664 | tf_op jit(solution)/shard_map/ppermute | solution.py:479
  359.9 13.3 %collective-permute-start.23 = (bf16[3,48,2304]{2,1,0:T(8,128)(2,1)S(1)}, bf16[3,48,2304]{2,1,0:T(8,128)(2,1)S(1)}, u32[]{:S(2)}, u32[]{:S(2)}) collective-permute-start(bf16[3,48,2304]{2,1,0:T(8,128)(2,1)S(1)} %collective-permute-done.10.refs_2_), channel_id=1, source_target_pairs={{0,1},{1,0},{2,3},{3,2},{4,5},{5,4},{6,7},{7,6},{8,9},{9,8},{10,11... | collective-permute-start | bytes 1990664 | tf_op jit(solution)/shard_map/ppermute | solution.py:479
  361.7 12.5 %collective-permute-start.22 = (bf16[3,48,2304]{2,1,0:T(8,128)(2,1)S(1)}, bf16[3,48,2304]{2,1,0:T(8,128)(2,1)S(1)}, u32[]{:S(2)}, u32[]{:S(2)}) collective-permute-start(bf16[3,48,2304]{2,1,0:T(8,128)(2,1)S(1)} %collective-permute-done.2.refs_0_), channel_id=1, source_target_pairs={{0,1},{1,0},{2,3},{3,2},{4,5},{5,4},{6,7},{7,6},{8,9},{9,8},{10,11... | collective-permute-start | bytes 1990664 | tf_op jit(solution)/shard_map/ppermute | solution.py:479
  363.7 13.4 %collective-permute-start.13 = (bf16[3,48,2304]{2,1,0:T(8,128)(2,1)S(1)}, bf16[3,48,2304]{2,1,0:T(8,128)(2,1)}, u32[]{:S(2)}, u32[]{:S(2)}) collective-permute-start(bf16[3,48,2304]{2,1,0:T(8,128)(2,1)S(1)} %collective-permute-done.12.refs_2_), channel_id=1, source_target_pairs={{0,14},{1,15},{2,0},{3,1},{4,2},{5,3},{6,4},{7,5},{8,6},{9,7},{10,... | collective-permute-start | bytes 1990664 | tf_op jit(solution)/shard_map/ppermute | solution.py:478
  367.1 13.5 %collective-permute-start.5 = (bf16[3,48,2304]{2,1,0:T(8,128)(2,1)}, bf16[3,48,2304]{2,1,0:T(8,128)(2,1)}, u32[]{:S(2)}, u32[]{:S(2)}) collective-permute-start(bf16[3,48,2304]{2,1,0:T(8,128)(2,1)} %collective-permute-done.4.refs_0_), channel_id=1, source_target_pairs={{0,2},{1,3},{2,4},{3,5},{4,6},{5,7},{6,8},{7,9},{8,10},{9,11},{10,... | collective-permute-start | bytes 1990664 | tf_op jit(solution)/shard_map/ppermute | solution.py:477
  368.0 14.3 %collective-permute-start.21 = (bf16[3,48,2304]{2,1,0:T(8,128)(2,1)S(1)}, bf16[3,48,2304]{2,1,0:T(8,128)(2,1)}, u32[]{:S(2)}, u32[]{:S(2)}) collective-permute-start(bf16[3,48,2304]{2,1,0:T(8,128)(2,1)S(1)} %collective-permute-done.11.refs_2_), channel_id=1, source_target_pairs={{0,1},{1,0},{2,3},{3,2},{4,5},{5,4},{6,7},{7,6},{8,9},{9,8},{10,11... | collective-permute-start | bytes 1990664 | tf_op jit(solution)/shard_map/ppermute | solution.py:479
  374.1 15.0 %collective-permute-start.20 = (bf16[3,48,2304]{2,1,0:T(8,128)(2,1)S(1)}, bf16[3,48,2304]{2,1,0:T(8,128)(2,1)}, u32[]{:S(2)}, u32[]{:S(2)}) collective-permute-start(bf16[3,48,2304]{2,1,0:T(8,128)(2,1)S(1)} %collective-permute-done.3.refs_0_), channel_id=1, source_target_pairs={{0,1},{1,0},{2,3},{3,2},{4,5},{5,4},{6,7},{7,6},{8,9},{9,8},{10,11... | collective-permute-start | bytes 1990664 | tf_op jit(solution)/shard_map/ppermute | solution.py:479
  375.0 14.3 %collective-permute-start.19 = (bf16[3,48,2304]{2,1,0:T(8,128)(2,1)S(1)}, bf16[3,48,2304]{2,1,0:T(8,128)(2,1)}, u32[]{:S(2)}, u32[]{:S(2)}) collective-permute-start(bf16[3,48,2304]{2,1,0:T(8,128)(2,1)S(1)} %collective-permute-done.12.refs_2_), channel_id=1, source_target_pairs={{0,1},{1,0},{2,3},{3,2},{4,5},{5,4},{6,7},{7,6},{8,9},{9,8},{10,11... | collective-permute-start | bytes 1990664 | tf_op jit(solution)/shard_map/ppermute | solution.py:479
  377.0 13.5 %collective-permute-start.14 = (bf16[3,48,2304]{2,1,0:T(8,128)(2,1)}, bf16[3,48,2304]{2,1,0:T(8,128)(2,1)}, u32[]{:S(2)}, u32[]{:S(2)}) collective-permute-start(bf16[3,48,2304]{2,1,0:T(8,128)(2,1)} %collective-permute-done.13.refs_2_), channel_id=1, source_target_pairs={{0,14},{1,15},{2,0},{3,1},{4,2},{5,3},{6,4},{7,5},{8,6},{9,7},{10,... | collective-permute-start | bytes 1990664 | tf_op jit(solution)/shard_map/ppermute | solution.py:478
  380.6 16.3 %collective-permute-start.6 = (bf16[3,48,2304]{2,1,0:T(8,128)(2,1)}, bf16[3,48,2304]{2,1,0:T(8,128)(2,1)}, u32[]{:S(2)}, u32[]{:S(2)}) collective-permute-start(bf16[3,48,2304]{2,1,0:T(8,128)(2,1)} %collective-permute-done.5.refs_0_), channel_id=1, source_target_pairs={{0,2},{1,3},{2,4},{3,5},{4,6},{5,7},{6,8},{7,9},{8,10},{9,11},{10,... | collective-permute-start | bytes 1990664 | tf_op jit(solution)/shard_map/ppermute | solution.py:477
  382.3 81.5 %collective-permute-start.18 = (bf16[3,48,2304]{2,1,0:T(8,128)(2,1)}, bf16[3,48,2304]{2,1,0:T(8,128)(2,1)}, u32[]{:S(2)}, u32[]{:S(2)}) collective-permute-start(bf16[3,48,2304]{2,1,0:T(8,128)(2,1)} %collective-permute-done.4.refs_0_), channel_id=1, source_target_pairs={{0,1},{1,0},{2,3},{3,2},{4,5},{5,4},{6,7},{7,6},{8,9},{9,8},{10,11... | collective-permute-start | bytes 1990664 | tf_op jit(solution)/shard_map/ppermute | solution.py:479
  389.1 86.4 %collective-permute-start.17 = (bf16[3,48,2304]{2,1,0:T(8,128)(2,1)}, bf16[3,48,2304]{2,1,0:T(8,128)(2,1)}, u32[]{:S(2)}, u32[]{:S(2)}) collective-permute-start(bf16[3,48,2304]{2,1,0:T(8,128)(2,1)} %collective-permute-done.13.refs_2_), channel_id=1, source_target_pairs={{0,1},{1,0},{2,3},{3,2},{4,5},{5,4},{6,7},{7,6},{8,9},{9,8},{10,11... | collective-permute-start | bytes 1990664 | tf_op jit(solution)/shard_map/ppermute | solution.py:479
  389.3 86.3 %collective-permute-start.16 = (bf16[3,48,2304]{2,1,0:T(8,128)(2,1)}, bf16[3,48,2304]{2,1,0:T(8,128)(2,1)}, u32[]{:S(2)}, u32[]{:S(2)}) collective-permute-start(bf16[3,48,2304]{2,1,0:T(8,128)(2,1)} %collective-permute-done.5.refs_0_), channel_id=1, source_target_pairs={{0,1},{1,0},{2,3},{3,2},{4,5},{5,4},{6,7},{7,6},{8,9},{9,8},{10,11... | collective-permute-start | bytes 1990664 | tf_op jit(solution)/shard_map/ppermute | solution.py:479
  390.5 97.1 %collective-permute-start.15 = (bf16[3,48,2304]{2,1,0:T(8,128)(2,1)}, bf16[3,48,2304]{2,1,0:T(8,128)(2,1)}, u32[]{:S(2)}, u32[]{:S(2)}) collective-permute-start(bf16[3,48,2304]{2,1,0:T(8,128)(2,1)} %collective-permute-done.14.refs_2_), channel_id=1, source_target_pairs={{0,1},{1,0},{2,3},{3,2},{4,5},{5,4},{6,7},{7,6},{8,9},{9,8},{10,11... | collective-permute-start | bytes 1990664 | tf_op jit(solution)/shard_map/ppermute | solution.py:479
  396.9 90.7 %collective-permute-start.7 = (bf16[3,48,2304]{2,1,0:T(8,128)(2,1)}, bf16[3,48,2304]{2,1,0:T(8,128)(2,1)}, u32[]{:S(2)}, u32[]{:S(2)}) collective-permute-start(bf16[3,48,2304]{2,1,0:T(8,128)(2,1)} %collective-permute-done.6.refs_0_), channel_id=1, source_target_pairs={{0,1},{1,0},{2,3},{3,2},{4,5},{5,4},{6,7},{7,6},{8,9},{9,8},{10,11... | collective-permute-start | bytes 1990664 | tf_op jit(solution)/shard_map/ppermute | solution.py:479
  (34 other events, 150.8 us)
where the time goes:
time: 507 us; the launch traced here: 500 us
  Pallas kernels  371 us (73%)
  starting transfers between devices  53.7 us (11%)
  waiting for transfers between devices  44.3 us (9%)
  local copies, waits for them, and re-layouts  27.9 us (6%)
    pallas_call x8, Pallas kernels, adam(): pl.pallas_call(functools.partial(adam_kernel, first), out_shape=shapes, g...  92.1 us
    pallas_call x1, Pallas kernels, first_layer(): pl.pallas_call(functools.partial(first_kernel, n, block), out_shape=(jax....  77.6 us
    pallas_call x1, Pallas kernels, summed(): pl.pallas_call(functools.partial(ring_kernel, n), out_shape=(jax.ShapeDty...  75.9 us
    pallas_call x2, Pallas kernels, by_weights(): pl.pallas_call(weight_kernel, out_shape=(jax.ShapeDtypeStruct((d, ff), BF...  62.3 us
    ppermute x7, waiting for transfers between devices, step(): left = lax.ppermute(left, 'dp', behind)  44.3 us
    pallas_call x1, Pallas kernels, last_layer(): pl.pallas_call(last_kernel, out_shape=(jax.ShapeDtypeStruct((tokens, d),...  31.6 us
    unnamed x80, local copies, waits for them, and re-layouts  27.6 us
    pallas_call x1, Pallas kernels, forward_up(): pl.pallas_call(up_kernel, out_shape=(jax.ShapeDtypeStruct((tokens, d), BF...  20.2 us
  transfers between devices with their start and end apart: 30, of which 7 were waited for; matrix products, arithmetic and copies ran while one was open for 0% of the time, Pallas kernels for 16%

commit v1 on v0

v1 whole, which is shorter than its diff:
```python
import functools

import jax
import jax.numpy as jnp
from jax import lax
from jax.experimental import pallas as pl
from jax.experimental.pallas import tpu as pltpu
from jax.sharding import PartitionSpec as P

MESH = pl.DeviceIdType.MESH
F32, BF16 = jnp.float32, jnp.bfloat16
EVERY = pl.BlockSpec(memory_space=pl.ANY)
VMEM = pl.BlockSpec(memory_space=pltpu.VMEM)


def rounded(a, b, contract=((1,), (0,))):
    return lax.dot_general(a, b, (contract, ((), ())), preferred_element_type=F32).astype(BF16)


def wide_dot(a, b):
    return jnp.dot(a, b, preferred_element_type=F32)


def scale_of(wide):
    return lax.rsqrt(jnp.mean(wide * wide, -1, keepdims=True) + 1e-6)


def normed(h):
    wide = h.astype(F32)
    return (wide * scale_of(wide)).astype(BF16)


def gated(gate, up):
    return (gate * jax.nn.sigmoid(gate) * up).astype(BF16)


def gated_back(gate, up, by_mid):
    by_mid = by_mid.astype(F32)
    one = jax.nn.sigmoid(gate)
    silu = gate * one
    by_gate = by_mid * up * (one * (1.0 + gate * (1.0 - one)))
    return (silu * up).astype(BF16), by_gate.astype(BF16), (by_mid * silu).astype(BF16)


def params(mib, **more):
    return pltpu.CompilerParams(vmem_limit_bytes=mib << 20, **more)


def cost(matmuls, tokens, d, ff, moved):
    return pl.CostEstimate(flops=2 * matmuls * tokens * d * ff, bytes_accessed=moved, transcendentals=tokens * ff)


def up_kernel(h_ref, gate_ref, up_ref, a_ref, mid_ref):
    @pl.when(pl.program_id(1) == 0)
    def _():
        a_ref[...] = normed(h_ref[...])

    a = a_ref[...]
    mid_ref[...] = gated(wide_dot(a, gate_ref[0]), wide_dot(a, up_ref[0]))


def columns_of(number, d, block):
    return pl.BlockSpec((1, d, block), lambda i, k: (number, 0, k))


def rows_of(number, d, block):
    return pl.BlockSpec((1, block, d), lambda i, k: (number, k, 0))


def forward_up(number, h, w_gate, w_up, tall=1024, block=768):
    tokens, d = h.shape
    ff = w_gate.shape[2]
    rows = pl.BlockSpec((tall, d), lambda i, k: (i, 0))
    part = pl.BlockSpec((tall, block), lambda i, k: (i, k))
    return pl.pallas_call(
        up_kernel,
        out_shape=(jax.ShapeDtypeStruct((tokens, d), BF16), jax.ShapeDtypeStruct((tokens, ff), BF16)),
        grid=(tokens // tall, ff // block),
        in_specs=[rows, columns_of(number, d, block), columns_of(number, d, block)],
        out_specs=(rows, part),
        compiler_params=params(63),
        cost_estimate=cost(2, tokens, d, ff, 26 << 20),
        name="forward_up",
    )(h, w_gate, w_up)


def down_kernel(mid_ref, down_ref, h_ref, out_ref):
    out_ref[...] = h_ref[...] + rounded(mid_ref[...], down_ref[0])


def forward_down(number, mid, w_down, h, tall=512):
    tokens, d = h.shape
    ff = mid.shape[1]
    rows = pl.BlockSpec((tall, d), lambda i: (i, 0))
    return pl.pallas_call(
        down_kernel,
        out_shape=jax.ShapeDtypeStruct((tokens, d), BF16),
        grid=(tokens // tall,),
        in_specs=[pl.BlockSpec((tall, ff), lambda i: (i, 0)), pl.BlockSpec((1, ff, d), lambda i: (number, 0, 0)), rows],
        out_specs=rows,
        compiler_params=params(63),
        cost_estimate=cost(1, tokens, d, ff, 20 << 20),
        name="forward_down",
    )(mid, w_down, h)


def last_kernel(h_ref, by_ref, gate_ref, up_ref, down_ref, a_ref, all_ref):
    @pl.when(pl.program_id(1) == 0)
    def _():
        a_ref[...] = normed(h_ref[...])

    a = a_ref[...]
    by_mid = rounded(by_ref[...], down_ref[0], ((1,), (1,)))
    all_ref[2], all_ref[0], all_ref[1] = gated_back(wide_dot(a, gate_ref[0]), wide_dot(a, up_ref[0]), by_mid)


def last_layer(number, h, by, w_gate, w_up, w_down, tall=1024, block=768):
    tokens, d = h.shape
    ff = w_gate.shape[2]
    rows = pl.BlockSpec((tall, d), lambda i, k: (i, 0))
    return pl.pallas_call(
        last_kernel,
        out_shape=(
            jax.ShapeDtypeStruct((tokens, d), BF16),
            jax.ShapeDtypeStruct((3, tokens, ff), BF16),
        ),
        grid=(tokens // tall, ff // block),
        in_specs=[rows, rows, columns_of(number, d, block), columns_of(number, d, block), rows_of(number, d, block)],
        out_specs=(rows, pl.BlockSpec((3, tall, block), lambda i, k: (0, i, k))),
        compiler_params=params(63),
        cost_estimate=cost(3, tokens, d, ff, 60 << 20),
        name="last_layer",
    )(h, by, w_gate, w_up, w_down)


def turn(a_ref, by_ref, turned):
    turned[0] = a_ref[...].T
    turned[1] = by_ref[...].T


def part_specs(tokens, d, ff, block):
    count = ff // block
    whole = pl.BlockSpec((tokens, d), lambda k: (0, 0), pipeline_mode=pl.Buffered(1))
    mid = pl.BlockSpec((tokens, block), lambda k: (0, jnp.minimum(k, count - 1)))
    both = pl.BlockSpec((1, tokens, block), lambda k: (jnp.maximum(k - count, 0) // count, 0, jnp.maximum(k - count, 0) % count))
    return [whole, whole, mid, both]


def weight_kernel(a_ref, by_ref, all_ref, wide_ref, down_ref, turned):
    now = pl.program_id(0)
    tall = now < pl.num_programs(0) // 3

    @pl.when(now == 0)
    def _():
        turn(a_ref, by_ref, turned)

    value = rounded(turned[jnp.where(tall, 1, 0)], all_ref[0])

    @pl.when(tall)
    def _():
        down_ref[...] = value.T

    @pl.when(jnp.logical_not(tall))
    def _():
        wide_ref[0] = value


def by_weights(a, by, every, block=768):
    tokens, d = a.shape
    ff = every.shape[2]
    count = ff // block
    whole, _, _, both = part_specs(tokens, d, ff, block)
    stacked = pl.BlockSpec((1, tokens, block), lambda k: (jnp.where(k < count, 2, k // count - 1), 0, k % count))
    return pl.pallas_call(
        weight_kernel,
        out_shape=(jax.ShapeDtypeStruct((2, d, ff), BF16), jax.ShapeDtypeStruct((ff, d), BF16)),
        grid=(3 * count,),
        in_specs=[whole, whole, stacked],
        out_specs=(pl.BlockSpec((1, d, block), both.index_map), pl.BlockSpec((block, d), lambda k: (jnp.minimum(k, count - 1), 0))),
        scratch_shapes=[pltpu.VMEM((2, d, tokens), BF16)],
        compiler_params=params(63, dimension_semantics=("arbitrary",)),
        cost_estimate=cost(3, tokens, d, ff, 45 << 20),
        name="by_weights",
    )(a, by, every)


def when(condition):
    if isinstance(condition, bool):
        return (lambda body: body()) if condition else (lambda body: None)
    return pl.when(condition)


class Ring:
    def __init__(self, n, grads, refs):
        self.n, self.chips, self.grads = n, n // 2, grads
        self.wide_own, self.wide_pair, self.wide_ring, self.tall_own, self.tall_pair, self.tall_ring = refs[:6]
        self.local, self.pair_send, self.pair_recv, self.ring_send, self.ring_recv = refs[6:]
        self.me = lax.axis_index("dp")
        self.z, self.c = self.me // 2, lax.rem(self.me, 2)
        self.partner = self.z * 2 + 1 - self.c
        self.beside = [lax.rem(self.z + k, self.chips) * 2 + self.c for k in (1, self.chips - 1)]

    @staticmethod
    def scratch(n, wide, tall, all_own):
        chips, sem = n // 2, pltpu.SemaphoreType.DMA
        own = n if all_own else chips
        bands = tall[0]
        return [
            pltpu.VMEM((2, own, *wide), BF16),
            pltpu.VMEM((2, chips, *wide), BF16),
            pltpu.VMEM((2, chips - 1, *wide), BF16),
            pltpu.VMEM((own * bands, *tall[1:]), BF16),
            pltpu.VMEM((chips * bands, *tall[1:]), BF16),
            pltpu.VMEM(((chips - 1) * bands, *tall[1:]), BF16),
            sem((3, chips)), sem((3, chips)), sem((3, chips)), sem((3, 2, chips - 1)), sem((3, 2, chips - 1)),
        ]

    def chunk(self, way, step):
        return lax.rem(self.z + (self.chips - 1 - step if way == 0 else 1 + step), self.chips)

    def at(self, i, wide, tall, j):
        if i < 2:
            return wide.at[i, j]
        bands = self.tall_ring.shape[0] // (self.chips - 1)
        return tall.at[pl.ds(j * bands, bands)]

    def own(self, i, j, theirs=False):
        if self.grads is None:
            j = 2 * j + (1 - self.c if theirs else self.c)
        return self.at(i, self.wide_own, self.tall_own, j)

    def pair(self, i, j):
        return self.at(i, self.wide_pair, self.tall_pair, j)

    def arriving(self, i, step):
        return self.at(i, self.wide_ring, self.tall_ring, step)

    def exchange(self, i, j):
        theirs = self.own(i, j, True) if self.grads is None else self.grads[i].at[j, 1 - self.c]
        away = pltpu.make_async_remote_copy(
            src_ref=theirs, dst_ref=self.pair(i, j), send_sem=self.pair_send.at[i, j], recv_sem=self.pair_recv.at[i, j],
            device_id={"dp": self.partner}, device_id_type=MESH,
        )
        if self.grads is None:
            return [away]
        return [away, pltpu.make_async_copy(self.grads[i].at[j, self.c], self.own(i, j), self.local.at[i, j])]

    def greet(self, everyone):
        barrier = pltpu.get_barrier_semaphore()
        others = [lax.rem(self.me + k, self.n) for k in range(1, self.n)] if everyone else [self.partner, *self.beside]
        for other in others:
            pl.semaphore_signal(barrier, inc=1, device_id={"dp": other}, device_id_type=MESH)
        pl.semaphore_wait(barrier, len(others))

    def begin(self, matrices):
        half = self.chips // 2
        for step in range(half):
            for way in range(2 if step < half - 1 else 1):
                for i in matrices:
                    for copy in self.exchange(i, self.chunk(way, step)):
                        copy.start()
        for i in matrices:
            for copy in self.exchange(i, self.z):
                copy.start()

    def ready(self, i, step):
        half = self.chips // 2

        @when(step < half)
        def _():
            for copy in self.exchange(i, self.chunk(0, step)):
                copy.wait()

        @when(step < half - 1)
        def _():
            for copy in self.exchange(i, self.chunk(1, step)):
                copy.wait()

    def half(self, i, way):
        columns = self.pair(i, 0).shape[-1] // 2
        return (slice(None),) * (1 if i < 2 else 2) + (slice(columns * way, columns * (way + 1)),)

    def hop(self, i, way, step):
        at = self.half(i, way)
        return pltpu.make_async_remote_copy(
            src_ref=self.own(i, self.chunk(way, step)).at[at], dst_ref=self.arriving(i, step).at[at],
            send_sem=self.ring_send.at[i, way, step], recv_sem=self.ring_recv.at[i, way, step],
            device_id={"dp": self.beside[way]}, device_id_type=MESH,
        )

    def add(self, i, way, j, step):
        own, pair, columns = self.own(i, j), self.pair(i, j), self.half(i, way)[-1]
        ring = None if step is None else self.arriving(i, step - 1)

        @pl.loop(0, 3)
        def _(part):
            deep = own.shape[0] // 3
            at = (pl.ds(pl.multiple_of(part * deep, deep), deep), columns) if i < 2 else (pl.ds(part * deep, deep), slice(None), columns)
            value = own[at].astype(F32) + pair[at].astype(F32)
            if ring is not None:
                value = value + ring[at].astype(F32)
            own[at] = value.astype(BF16)

    def send(self, i, step):
        self.ready(i, step)

        @when(step == 0)
        def _():
            for way in range(2):
                self.add(i, way, self.chunk(way, step), None)

        @when(step > 0)
        def _():
            for way in range(2):
                self.hop(i, way, step - 1).wait_recv()
                self.add(i, way, self.chunk(way, step), step)

        for way in range(2):
            self.hop(i, way, step).start()

    def finish(self, i, out):
        last = self.chips - 1
        for copy in self.exchange(i, self.z):
            copy.wait()
        for way in range(2):
            self.hop(i, way, last - 1).wait_recv()
            self.add(i, way, self.z, last)
        own = self.own(i, self.z)
        if i < 2:
            out[i] = own[...]
        else:
            bands, _, columns = own.shape
            for k in range(bands):
                out[i, :, columns * k : columns * (k + 1)] = own[k]

    def drain(self):
        for i in range(3):
            for way in range(2):

                @pl.loop(0, self.chips - 1)
                def _(step):
                    self.hop(i, way, step).wait_send()


def squares_of(ref):
    squares = jnp.zeros((8, 128), F32)
    for i in range(ref.shape[0]):
        value = ref[i].astype(F32)
        flat = jnp.sum((value * value).reshape(-1, 8, value.shape[1]), axis=0)
        for k in range(flat.shape[1] // 128):
            squares = squares + flat[:, 128 * k : 128 * (k + 1)]
    return squares


def weight_ring_kernel(n, *refs):
    a_ref, by_ref, mid_ref, by_both_ref, before_ref, out_ref, ss_ref, turned, parts, ss_send, ss_recv = refs[:11]
    ring = Ring(n, None, refs[11:])
    block, rest = mid_ref.shape[1], ring.chips - 1
    columns = ring.wide_own.shape[3] // block
    now = pl.program_id(0)
    me = ring.me

    @pl.when(now == 0)
    def _():
        ring.greet(True)
        parts[me] = squares_of(before_ref)
        turn(a_ref, by_ref, turned)

    @pl.when(now == columns)
    def _():
        ring.begin([2])

    @pl.when(now == 2 * columns)
    def _():
        ring.begin([0])

    @pl.when(now > columns)
    def _():
        ring.send(2, now - columns - 1)

    @pl.when(now > 2 * columns)
    def _():
        ring.send(0, now - 2 * columns - 1)

    @pl.when(now < columns)
    def _():
        value = rounded(turned[1], mid_ref[...]).T
        bands = block // ring.tall_own.shape[1]
        ring.tall_own[pl.ds(now * bands, bands)] = value.reshape(bands, -1, value.shape[1])

    @pl.when(now >= columns)
    def _():
        value = rounded(turned[0], by_both_ref[0]).reshape(n, -1, block)
        at = pl.ds(pl.multiple_of(lax.rem(now, columns) * block, block), block)
        ring.wide_own[now // columns - 1, :, :, at] = value

    @pl.when(now == 3 * columns - 1)
    def _():
        gate, down = columns - 1, 2 * columns - 1
        ring.begin([1])

        @pl.loop(0, rest)
        def _(step):
            @pl.when(gate + step < rest)
            def _():
                ring.send(0, gate + step)

            @pl.when(down + step < rest)
            def _():
                ring.send(2, down + step)

            ring.send(1, step)

        for i in (2, 0, 1):
            ring.finish(i, out_ref)
        parts[me] = parts[me] + squares_of(out_ref)
        ring.drain()

        def tell(k):
            return pltpu.make_async_remote_copy(
                src_ref=parts.at[me], dst_ref=parts.at[me], send_sem=ss_send.at[k], recv_sem=ss_recv.at[k],
                device_id={"dp": lax.rem(me + k, n)}, device_id_type=MESH,
            )

        for k in range(1, n):
            tell(k).start()
        for k in range(1, n):
            tell(k).wait()
        everyone = parts[0]
        for k in range(1, n):
            everyone = everyone + parts[k]
        ss_ref[...] = everyone


def shapes_of(n, d, ff):
    return (d // n, ff), (ff // d, d // n, d)


def weights_summed(n, a, by, mid, by_both, before, block=768):
    tokens, d = a.shape
    ff = mid.shape[1]
    wide, tall = shapes_of(n, d, ff)
    return pl.pallas_call(
        functools.partial(weight_ring_kernel, n),
        out_shape=(jax.ShapeDtypeStruct((3, *wide), BF16), jax.ShapeDtypeStruct((8, 128), F32)),
        grid=(3 * ff // block,),
        in_specs=[*part_specs(tokens, d, ff, block), pl.BlockSpec((3, *wide), lambda k: (0, 0, 0))],
        out_specs=(pl.BlockSpec((3, *wide), lambda k: (0, 0, 0)), pl.BlockSpec((8, 128), lambda k: (0, 0))),
        scratch_shapes=[
            pltpu.VMEM((2, d, tokens), BF16), pltpu.VMEM((n, 8, 128), F32), pltpu.SemaphoreType.DMA((n,)), pltpu.SemaphoreType.DMA((n,)),
            *Ring.scratch(n, wide, tall, True),
        ],
        compiler_params=params(63, collective_id=0, has_side_effects=True, dimension_semantics=("arbitrary",)),
        cost_estimate=cost(3, tokens, d, ff, 45 << 20),
        name="weights_summed",
    )(a, by, mid, by_both, before)


def first_kernel(n, block, *refs):
    wide_grads, tall_grads, w_gate, w_up, w_down, by_both1, h1, by1, a0 = refs[:9]
    out_ref, by_ref, by_both_ref, gate1, up1, gate0, up0, down0, fetched = refs[9:18]
    ring = Ring(n, [wide_grads.at[0], wide_grads.at[1], tall_grads], refs[18:])
    rest = ring.chips - 1
    tile = pl.program_id(0)
    moved = ((w_gate, 1, gate1), (w_up, 1, up1), (w_down, 0, down0), (w_gate, 0, gate0), (w_up, 0, up0))
    fetches = [pltpu.make_async_copy(w.at[number], to, fetched.at[k]) for k, (w, number, to) in enumerate(moved)]

    @pl.when(tile == 0)
    def _():
        for fetch in fetches:
            fetch.start()
        ring.greet(False)
        ring.begin([0, 1, 2])

    def have(*which):
        @pl.when(tile == 0)
        def _():
            for k in which:
                fetches[k].wait()

    def moment(which):
        step, i = 2 * tile + which // 3, which % 3

        @pl.when(step < rest)
        def _():
            ring.send(i, step)

        if which >= 3:

            @pl.when(step == rest)
            def _():
                ring.finish(i, out_ref)

    last = ((1,), (1,))
    have(0)
    by_gate_part = rounded(by_both1[0], gate1[...], last)
    moment(0)
    have(1)
    by_a = by_gate_part + rounded(by_both1[1], up1[...], last)
    wide, by_a = h1[...].astype(F32), by_a.astype(F32)
    scale = scale_of(wide)
    dots = jnp.sum(by_a * wide, -1, keepdims=True) / wide.shape[1]
    by_ref[...] = by1[...] + (by_a * scale - wide * (scale * scale * scale * dots)).astype(BF16)
    moment(1)
    have(2, 3, 4)

    @pl.loop(0, gate0.shape[1] // block)
    def _(k):
        at = pl.ds(pl.multiple_of(block * k, block), block)
        a = a0[...]
        by_mid = rounded(by_ref[...], down0[at, :], last)
        _, by_both_ref[0, :, at], by_both_ref[1, :, at] = gated_back(wide_dot(a, gate0[:, at]), wide_dot(a, up0[:, at]), by_mid)
        for part in range(3):

            @pl.when(k == part)
            def _():
                moment(2 + part)

    moment(5)

    @pl.when(tile == pl.num_programs(0) - 1)
    def _():
        ring.drain()


def first_layer(n, grads, by_both, h, by, a, w_gate, w_up, w_down, block=768):
    tokens, d = h.shape
    ff = by_both.shape[2]
    wide, tall = shapes_of(n, d, ff)
    deep = tokens // (n // 4)

    rows, both = pl.BlockSpec((deep, d), lambda i: (i, 0)), pl.BlockSpec((2, deep, ff), lambda i: (0, i, 0))
    return pl.pallas_call(
        functools.partial(first_kernel, n, block),
        out_shape=(
            jax.ShapeDtypeStruct((3, *wide), BF16),
            jax.ShapeDtypeStruct((tokens, d), BF16),
            jax.ShapeDtypeStruct((2, tokens, ff), BF16),
        ),
        grid=(n // 4,),
        in_specs=[EVERY] * 5 + [both, rows, rows, rows],
        out_specs=(pl.BlockSpec((3, *wide), lambda i: (0, 0, 0)), rows, both),
        scratch_shapes=[
            *(pltpu.VMEM(shape, BF16) for shape in ((d, ff), (d, ff), (d, ff), (d, ff), (ff, d))), pltpu.SemaphoreType.DMA((5,)),
            *Ring.scratch(n, wide, tall, False),
        ],
        compiler_params=params(63, collective_id=1, has_side_effects=True, dimension_semantics=("arbitrary",)),
        cost_estimate=cost(5, tokens, d, ff, 60 << 20),
        name="first_layer",
    )(
        grads[0].reshape(2, n // 2, 2, *wide), grads[1].reshape(n // 2, 2, *tall),
        w_gate, w_up, w_down, by_both, h, by, a,
    )


def adam_kernel(first, where_ref, factor_ref, *refs):
    pieces, (w, m, v) = refs[:4], (refs[4:7], refs[7:10], refs[10:13])
    new_w, new_m, new_v = (refs[i : i + 3] for i in ((13, 16, 19) if first else (22, 25, 28)))
    g_ref = refs[-1]
    part = pl.program_id(0)
    for p in range(4):

        @pl.when(part == p)
        def _():
            g_ref[...] = pieces[p][...]

    factor = factor_ref[0]
    for which in range(3):
        rows, columns = w[which].shape[1:]
        deep = g_ref.shape[1]
        for k in range(rows // deep):

            @pl.loop(0, deep // 16)
            def _(strip):
                at = (0, pl.ds(pl.multiple_of(deep * k + strip * 16, 16), 16), slice(None))
                g = g_ref[which, pl.ds(pl.multiple_of(strip * 16, 16), 16), columns * k : columns * (k + 1)].astype(F32) * factor
                mean = 0.9 * m[which][at] + 0.1 * g
                square = 0.95 * v[which][at] + 0.05 * g * g
                wide = w[which][at].astype(F32)
                new_m[which][at] = mean
                new_v[which][at] = square
                new_w[which][at] = (wide - 0.02 * (mean * lax.rsqrt(square + 1e-8) + 0.1 * wide)).astype(BF16)


def adam(n, where, factor, pieces, state, so_far):
    first = so_far is None
    shapes = [jax.ShapeDtypeStruct(s.shape, s.dtype) for s in state]

    def block(s):
        return pl.BlockSpec((1, s.shape[1] // n, s.shape[2]), lambda p, where, factor: (where[0, p], where[1, p], 0))

    whole = pl.BlockSpec(pieces[0].shape, lambda p, where, factor: (0, 0, 0))
    size = sum(s.size // n for s in state[:3]) * 4
    return pl.pallas_call(
        functools.partial(adam_kernel, first),
        out_shape=shapes,
        grid_spec=pltpu.PrefetchScalarGridSpec(
            num_scalar_prefetch=2,
            grid=(4,),
            in_specs=[whole] * 4 + [block(s) for s in state] + ([] if first else [EVERY] * 9),
            out_specs=[block(s) for s in state],
            scratch_shapes=[pltpu.VMEM(pieces[0].shape, BF16)],
        ),
        input_output_aliases={} if first else {15 + i: i for i in range(9)},
        compiler_params=params(48, dimension_semantics=("arbitrary",)),
        cost_estimate=pl.CostEstimate(flops=60_000_000, bytes_accessed=size * 11, transcendentals=size // 4),
        name="adam_step",
    )(where, factor, *pieces, *state, *(so_far or ()))


def solution(mesh):
    n = mesh.shape["dp"]
    chips = n // 2

    def step(x, dy, *arrays):
        weights, m, v = (arrays[i : i + 3] for i in (0, 3, 6))
        w_gate, w_up, w_down = weights
        x, dy = x[0], dy[0]
        a0, mid0 = forward_up(0, x, w_gate, w_up)
        h1 = forward_down(0, mid0, w_down, x)
        a1, all1 = last_layer(1, h1, dy, w_gate, w_up, w_down)
        grads1 = by_weights(a1, dy, all1)
        right, by, by_both0 = first_layer(n, grads1, all1, h1, dy, a0, w_gate, w_up, w_down)
        left, squares = weights_summed(n, a0, by, mid0, by_both0, right)
        count = sum(w.size for w in weights)
        factor = jnp.minimum(1.0, 0.5 * lax.rsqrt(jnp.sum(squares) / count + 1e-30)).reshape(1)

        me = lax.axis_index("dp")
        z, c = me // 2, me % 2
        ahead = [(i, (i + 2) % n) for i in range(n)]
        behind = [(i, (i + n - 2) % n) for i in range(n)]
        pairs = [(i, i ^ 1) for i in range(n)]
        new = None
        for hop in range(chips):
            if hop:
                right = lax.ppermute(right, "dp", ahead)
                left = lax.ppermute(left, "dp", behind)
            pieces = [right, lax.ppermute(right, "dp", pairs), left, lax.ppermute(left, "dp", pairs)]
            from_right, from_left = (z + chips - hop) % chips * 2, (z + hop) % chips * 2
            where = jnp.array([[1, 1, 0, 0], [0, 0, 0, 0]], jnp.int32).at[1].set(
                jnp.stack([from_right + c, from_right + 1 - c, from_left + c, from_left + 1 - c])
            )
            new = adam(n, where, factor, pieces, (*weights, *m, *v), new)
        return tuple(new)

    return jax.shard_map(
        step,
        mesh=mesh,
        in_specs=(P(("rep", "dp"), None, None),) * 2 + (P(None, None, None),) * 9,
        out_specs=(P("rep", None, None),) * 9,
        check_vma=False,
    )
```

time: 507 us -> 495 us (0.976)
  local copies, waits for them, and re-layouts: 27.9 us -> 14.9 us
    unnamed x80 -> x64, local copies, waits for them, and re-layouts: 27.6 us -> 14.7 us
    pallas_call x3 -> x2, Pallas kernels: 138 us -> 130 us  [the longest x1 96.8 us: weights_summed(): pl.pallas_call(functools.partial(weight_ring_kernel, n), out_shape=(jax.S...]
  transfers between devices with their start and end apart: 30 -> 30, of which waited for: 7 -> 7; matrix products, arithmetic and copies ran while one was open for 0% -> 0% of each run, Pallas kernels for 16% -> 17%
where the time goes in v1:
time: 495 us; the launch traced here: 486 us
  Pallas kernels  367 us (74%)
  starting transfers between devices  55.5 us (11%)
  waiting for transfers between devices  44.7 us (9%)
  local copies, waits for them, and re-layouts  14.9 us (3%)
    pallas_call x8, Pallas kernels, adam(): pl.pallas_call(functools.partial(adam_kernel, first), out_shape=shapes, g...  97 us
    pallas_call x1, Pallas kernels, weights_summed(): pl.pallas_call(functools.partial(weight_ring_kernel, n), out_shape=(jax.S...  96.8 us
    pallas_call x1, Pallas kernels, first_layer(): pl.pallas_call(functools.partial(first_kernel, n, block), out_shape=(jax....  74.7 us
    ppermute x7, waiting for transfers between devices, step(): left = lax.ppermute(left, 'dp', behind)  44.6 us
    pallas_call x1, Pallas kernels, by_weights(): pl.pallas_call(weight_kernel, out_shape=(jax.ShapeDtypeStruct((2, d, ff),...  32.9 us
    pallas_call x1, Pallas kernels, last_layer(): pl.pallas_call(last_kernel, out_shape=(jax.ShapeDtypeStruct((tokens, d),...  32.4 us
    ppermute x7, starting transfers between devices, step(): left = lax.ppermute(left, 'dp', behind)  21.4 us
    pallas_call x1, Pallas kernels, forward_up(): pl.pallas_call(up_kernel, out_shape=(jax.ShapeDtypeStruct((tokens, d), BF...  20.8 us
  transfers between devices with their start and end apart: 30, of which 7 were waited for; matrix products, arithmetic and copies ran while one was open for 0% of the time, Pallas kernels for 17%

profile of v1, /device:TPU:21, one launch (start us, length us, event | category | flops | bytes accessed | tf_op | source)
XLA Modules:
  0.0 486.3 jit_solution(16275131926886938894)
XLA Ops:
  0.6 20.8 %forward_up.1 = (bf16[2048,768]{1,0:T(8,128)(2,1)}, bf16[2048,2304]{1,0:T(8,128)(2,1)}) custom-call(bf16[2048,768]{1,0:T(8,128)(2,1)} %bitcast.39, bf16[2,768,2304]{2,1,0:T(8,128)(2,1)} %refs_4_.17, bf16[2,768,2304]{2,1,0:T(8,128)(2,1)} %refs_5_.15), custom_call_target="tpu_custom_call" | custom-call | flops 14495514624 | bytes 27262976 | tf_op jit(solution)/shard_map/forward_up/pallas_call | solution.py:75
  21.4 12.7 %forward_down.1.h_ref.refs_6_ = bf16[2048,768]{1,0:T(8,128)(2,1)} custom-call(bf16[2048,2304]{1,0:T(8,128)(2,1)} %get-tuple-element.180.mid_ref.refs_2_, bf16[2,2304,768]{2,1,0:T(8,128)(2,1)} %refs_6_.15, bf16[2048,768]{1,0:T(8,128)(2,1)} %bitcast.40), custom_call_target="tpu_custom_call" | custom-call | flops 7247757312 | bytes 20971520 | tf_op jit(solution)/shard_map/forward_down/pallas_call | solution.py:95
  34.1 32.4 %last_layer.1 = (bf16[2048,768]{1,0:T(8,128)(2,1)}, bf16[3,2048,2304]{2,1,0:T(8,128)(2,1)}) custom-call(bf16[2048,768]{1,0:T(8,128)(2,1)} %forward_down.1.h_ref.refs_6_, bf16[2048,768]{1,0:T(8,128)(2,1)} %bitcast.41, bf16[2,768,2304]{2,1,0:T(8,128)(2,1)} %refs_4_.17, bf16[2,768,2304]{2,1,0:T(8,128)(2,1)} %refs_5_.15, bf16[2,2304,768]{2,1,0:T(8,128)(2,1)} %refs_6_.15), custom_call_target="tpu_custom_call" | custom-call | flops 21743271936 | bytes 62914560 | tf_op jit(solution)/shard_map/last_layer/pallas_call | solution.py:121
  66.5 32.9 %by_weights.1 = (bf16[2,768,2304]{2,1,0:T(8,128)(2,1)}, bf16[2304,768]{1,0:T(8,128)(2,1)}) custom-call(bf16[2048,768]{1,0:T(8,128)(2,1)} %get-tuple-element.181.a_ref, bf16[2048,768]{1,0:T(8,128)(2,1)} %bitcast.42, bf16[3,2048,2304]{2,1,0:T(8,128)(2,1)} %get-tuple-element.182.all_ref.refs_5_), custom_call_target="tpu_custom_call" | custom-call | flops 21743271936 | bytes 47185920 | tf_op jit(solution)/shard_map/by_weights/pallas_call | solution.py:174
  99.4 74.7 %first_layer.1 = (bf16[3,48,2304]{2,1,0:T(8,128)(2,1)}, bf16[2048,768]{1,0:T(8,128)(2,1)}, bf16[2,2048,2304]{2,1,0:T(8,128)(2,1)}) custom-call(bf16[2,8,2,48,2304]{4,3,2,1,0:T(8,128)(2,1)} %bitcast.44, bf16[8,2,3,48,768]{4,3,2,1,0:T(8,128)(2,1)} %bitcast.45, bf16[2,768,2304]{2,1,0:T(8,128)(2,1)} %refs_4_.17, bf16[2,768,2304]{2,1,0:T(8,128)(2,1)} %refs_5_.15, ...), custom_call_target="tpu_custom_call" | custom-call | flops 36238786560 | bytes 62914560 | tf_op jit(solution)/shard_map/first_layer/pallas_call | solution.py:533
  174.1 96.8 %weights_summed.1 = (bf16[3,48,2304]{2,1,0:T(8,128)(2,1)}, f32[8,128]{1,0:T(8,128)}) custom-call(bf16[2048,768]{1,0:T(8,128)(2,1)} %get-tuple-element.179.refs_8_.refs_0_, bf16[2048,768]{1,0:T(8,128)(2,1)} %get-tuple-element.185.refs_1_, bf16[2048,2304]{1,0:T(8,128)(2,1)} %get-tuple-element.180.mid_ref.refs_2_, ...), custom_call_target="tpu_custom_call" | custom-call | flops 21743271936 | bytes 47185920 | tf_op jit(solution)/shard_map/weights_summed/pallas_call | solution.py:443
  270.9 1.6 collective-permute-start.8
  272.5 14.8 %collective-permute-done.8.refs_2_ = bf16[3,48,2304]{2,1,0:T(8,128)(2,1)S(1)} collective-permute-done((bf16[3,48,2304]{2,1,0:T(8,128)(2,1)}, bf16[3,48,2304]{2,1,0:T(8,128)(2,1)S(1)}, u32[]{:S(2)}, u32[]{:S(2)}) %collective-permute-start.8) | collective-permute-done | bytes 663584 | tf_op jit(solution)/shard_map/ppermute | solution.py:637
  287.3 2.7 collective-permute-start.9
  290.0 13.0 %collective-permute-done.9.refs_2_ = bf16[3,48,2304]{2,1,0:T(8,128)(2,1)S(1)} collective-permute-done((bf16[3,48,2304]{2,1,0:T(8,128)(2,1)S(1)}, bf16[3,48,2304]{2,1,0:T(8,128)(2,1)S(1)}, u32[]{:S(2)}, u32[]{:S(2)}) %collective-permute-start.9) | collective-permute-done | bytes 663584 | tf_op jit(solution)/shard_map/ppermute | solution.py:637
  303.0 3.4 collective-permute-start.10
  306.4 2.4 collective-permute-start.29
  308.9 9.6 %collective-permute-done.10.refs_2_ = bf16[3,48,2304]{2,1,0:T(8,128)(2,1)S(1)} collective-permute-done((bf16[3,48,2304]{2,1,0:T(8,128)(2,1)S(1)}, bf16[3,48,2304]{2,1,0:T(8,128)(2,1)S(1)}, u32[]{:S(2)}, u32[]{:S(2)}) %collective-permute-start.10) | collective-permute-done | bytes 663584 | tf_op jit(solution)/shard_map/ppermute | solution.py:637
  318.5 3.4 collective-permute-start.11
  322.0 3.2 collective-permute-start.27
  329.1 4.2 collective-permute-done.11.refs_2_
  333.2 3.4 collective-permute-start.12
  337.5 4.1 collective-permute-start.24
  347.1 3.4 collective-permute-start.13
  351.4 5.5 %collective-permute-start.21 = (bf16[3,48,2304]{2,1,0:T(8,128)(2,1)S(1)}, bf16[3,48,2304]{2,1,0:T(8,128)(2,1)}, u32[]{:S(2)}, u32[]{:S(2)}) collective-permute-start(bf16[3,48,2304]{2,1,0:T(8,128)(2,1)S(1)} %collective-permute-done.11.refs_2_), channel_id=1, source_target_pairs={{0,1},{1,0},{2,3},{3,2},{4,5},{5,4},{6,7},{7,6},{8,9},{9,8},{10,11... | collective-permute-start | bytes 1990664 | tf_op jit(solution)/shard_map/ppermute | solution.py:638
  360.5 3.5 collective-permute-start.14
  366.4 6.8 %collective-permute-start.18 = (bf16[3,48,2304]{2,1,0:T(8,128)(2,1)}, bf16[3,48,2304]{2,1,0:T(8,128)(2,1)}, u32[]{:S(2)}, u32[]{:S(2)}) collective-permute-start(bf16[3,48,2304]{2,1,0:T(8,128)(2,1)} %collective-permute-done.4.refs_0_), channel_id=1, source_target_pairs={{0,1},{1,0},{2,3},{3,2},{4,5},{5,4},{6,7},{7,6},{8,9},{9,8},{10,11... | collective-permute-start | bytes 1990664 | tf_op jit(solution)/shard_map/ppermute | solution.py:638
  373.9 6.4 %collective-permute-start.15 = (bf16[3,48,2304]{2,1,0:T(8,128)(2,1)}, bf16[3,48,2304]{2,1,0:T(8,128)(2,1)}, u32[]{:S(2)}, u32[]{:S(2)}) collective-permute-start(bf16[3,48,2304]{2,1,0:T(8,128)(2,1)} %collective-permute-done.14.refs_2_), channel_id=1, source_target_pairs={{0,1},{1,0},{2,3},{3,2},{4,5},{5,4},{6,7},{7,6},{8,9},{9,8},{10,11... | collective-permute-start | bytes 1990664 | tf_op jit(solution)/shard_map/ppermute | solution.py:638
  380.3 3.4 collective-permute-start.7
  388.8 11.7 %adam_step.8 = (bf16[2,768,2304]{2,1,0:T(8,128)(2,1)}, bf16[2,768,2304]{2,1,0:T(8,128)(2,1)}, bf16[2,2304,768]{2,1,0:T(8,128)(2,1)}, f32[2,768,2304]{2,1,0:T(8,1...) custom-call(s32[2,4]{1,0:T(2,128)S(1)} %scatter.39.where_ref, ...), custom_call_target="tpu_custom_call" | custom-call | flops 60000000 | bytes 29196288 | tf_op jit(solution)/shard_map/adam_step/pallas_call | solution.py:594
  400.6 11.8 %adam_step.9 = (bf16[2,768,2304]{2,1,0:T(8,128)(2,1)}, bf16[2,768,2304]{2,1,0:T(8,128)(2,1)}, bf16[2,2304,768]{2,1,0:T(8,128)(2,1)}, f32[2,768,2304]{2,1,0:T(8,1...) custom-call(s32[2,4]{1,0:T(2,128)S(1)} %scatter.36.where_ref, ...), custom_call_target="tpu_custom_call", output_to_operand_aliasing={{0}: (15, {}), {1}: (16, {}), {2}: (17, {}), {3}: (18, {}),... | custom-call | flops 60000000 | bytes 29196288 | tf_op jit(solution)/shard_map/adam_step/pallas_call | solution.py:594
  412.4 11.8 %adam_step.10 = (bf16[2,768,2304]{2,1,0:T(8,128)(2,1)}, bf16[2,768,2304]{2,1,0:T(8,128)(2,1)}, bf16[2,2304,768]{2,1,0:T(8,128)(2,1)}, f32[2,768,2304]{2,1,0:T(8,...) custom-call(s32[2,4]{1,0:T(2,128)S(1)} %scatter.35.where_ref, ...), custom_call_target="tpu_custom_call", output_to_operand_aliasing={{0}: (15, {}), {1}: (16, {}), {2}: (17, {}), {3}: (18, {}),... | custom-call | flops 60000000 | bytes 29196288 | tf_op jit(solution)/shard_map/adam_step/pallas_call | solution.py:594
  424.2 11.8 %adam_step.11 = (bf16[2,768,2304]{2,1,0:T(8,128)(2,1)}, bf16[2,768,2304]{2,1,0:T(8,128)(2,1)}, bf16[2,2304,768]{2,1,0:T(8,128)(2,1)}, f32[2,768,2304]{2,1,0:T(8,...) custom-call(s32[2,4]{1,0:T(2,128)S(1)} %scatter.34.where_ref, ...), custom_call_target="tpu_custom_call", output_to_operand_aliasing={{0}: (15, {}), {1}: (16, {}), {2}: (17, {}), {3}: (18, {}),... | custom-call | flops 60000000 | bytes 29196288 | tf_op jit(solution)/shard_map/adam_step/pallas_call | solution.py:594
  436.0 12.3 %adam_step.12 = (bf16[2,768,2304]{2,1,0:T(8,128)(2,1)}, bf16[2,768,2304]{2,1,0:T(8,128)(2,1)}, bf16[2,2304,768]{2,1,0:T(8,128)(2,1)}, f32[2,768,2304]{2,1,0:T(8,...) custom-call(s32[2,4]{1,0:T(2,128)S(1)} %scatter.31.where_ref, ...), custom_call_target="tpu_custom_call", output_to_operand_aliasing={{0}: (15, {}), {1}: (16, {}), {2}: (17, {}), {3}: (18, {}),... | custom-call | flops 60000000 | bytes 29196288 | tf_op jit(solution)/shard_map/adam_step/pallas_call | solution.py:594
  448.3 12.5 %adam_step.13 = (bf16[2,768,2304]{2,1,0:T(8,128)(2,1)}, bf16[2,768,2304]{2,1,0:T(8,128)(2,1)}, bf16[2,2304,768]{2,1,0:T(8,128)(2,1)}, f32[2,768,2304]{2,1,0:T(8,...) custom-call(s32[2,4]{1,0:T(2,128)S(1)} %scatter.30.where_ref, ...), custom_call_target="tpu_custom_call", output_to_operand_aliasing={{0}: (15, {}), {1}: (16, {}), {2}: (17, {}), {3}: (18, {}),... | custom-call | flops 60000000 | bytes 29196288 | tf_op jit(solution)/shard_map/adam_step/pallas_call | solution.py:594
  460.7 12.7 %adam_step.14 = (bf16[2,768,2304]{2,1,0:T(8,128)(2,1)}, bf16[2,768,2304]{2,1,0:T(8,128)(2,1)}, bf16[2,2304,768]{2,1,0:T(8,128)(2,1)}, f32[2,768,2304]{2,1,0:T(8,...) custom-call(s32[2,4]{1,0:T(2,128)S(1)} %scatter.29.where_ref, ...), custom_call_target="tpu_custom_call", output_to_operand_aliasing={{0}: (15, {}), {1}: (16, {}), {2}: (17, {}), {3}: (18, {}),... | custom-call | flops 60000000 | bytes 29196288 | tf_op jit(solution)/shard_map/adam_step/pallas_call | solution.py:594
  473.4 12.7 %adam_step.15 = (bf16[2,768,2304]{2,1,0:T(8,128)(2,1)}, bf16[2,768,2304]{2,1,0:T(8,128)(2,1)}, bf16[2,2304,768]{2,1,0:T(8,128)(2,1)}, f32[2,768,2304]{2,1,0:T(8,...) custom-call(s32[2,4]{1,0:T(2,128)S(1)} %scatter.26.where_ref, ...), custom_call_target="tpu_custom_call", output_to_operand_aliasing={{0}: (15, {}), {1}: (16, {}), {2}: (17, {}), {3}: (18, {}),... | custom-call | flops 60000000 | bytes 29196288 | tf_op jit(solution)/shard_map/adam_step/pallas_call | solution.py:594
  (123 shorter events, 22.1 us)
Async XLA Ops:
  174.1 98.4 %copy-start.4 = (bf16[3,48,2304]{2,1,0:T(8,128)(2,1)S(1)}, bf16[3,48,2304]{2,1,0:T(8,128)(2,1)}, u32[]{:S(2)}) copy-start(bf16[3,48,2304]{2,1,0:T(8,128)(2,1)} %get-tuple-element.187.refs_4_.refs_0_) | copy-start | bytes 1990660
  174.1 189.9 %copy-start.27 = (s32[2,4]{1,0:T(2,128)S(1)}, s32[2,4]{1,0:T(2,128)}, u32[]{:S(2)}) copy-start(s32[2,4]{1,0:T(2,128)} %constant.302.clone) | copy-start | bytes 100
  270.9 16.4 %collective-permute-start.8 = (bf16[3,48,2304]{2,1,0:T(8,128)(2,1)}, bf16[3,48,2304]{2,1,0:T(8,128)(2,1)S(1)}, u32[]{:S(2)}, u32[]{:S(2)}) collective-permute-start(bf16[3,48,2304]{2,1,0:T(8,128)(2,1)} %get-tuple-element.189.refs_2_), channel_id=1, source_target_pairs={{0,14},{1,15},{2,0},{3,1},{4,2},{5,3},{6,4},{7,5},{8,6},{9,7},{10,... | collective-permute-start | bytes 1990664 | tf_op jit(solution)/shard_map/ppermute | solution.py:637
  272.5 17.5 %collective-permute-start = (bf16[3,48,2304]{2,1,0:T(8,128)(2,1)S(1)}, bf16[3,48,2304]{2,1,0:T(8,128)(2,1)S(1)}, u32[]{:S(2)}, u32[]{:S(2)}) collective-permute-start(bf16[3,48,2304]{2,1,0:T(8,128)(2,1)S(1)} %copy-done.4), channel_id=1, source_target_pairs={{0,2},{1,3},{2,4},{3,5},{4,6},{5,7},{6,8},{7,9},{8,10},{9,11},{10,... | collective-permute-start | bytes 1990664 | tf_op jit(solution)/shard_map/ppermute | solution.py:636
  287.3 15.7 %collective-permute-start.9 = (bf16[3,48,2304]{2,1,0:T(8,128)(2,1)S(1)}, bf16[3,48,2304]{2,1,0:T(8,128)(2,1)S(1)}, u32[]{:S(2)}, u32[]{:S(2)}) collective-permute-start(bf16[3,48,2304]{2,1,0:T(8,128)(2,1)S(1)} %collective-permute-done.8.refs_2_), channel_id=1, source_target_pairs={{0,14},{1,15},{2,0},{3,1},{4,2},{5,3},{6,4},{7,5},{8,6},{9,7},{10,... | collective-permute-start | bytes 1990664 | tf_op jit(solution)/shard_map/ppermute | solution.py:637
  290.0 16.4 %collective-permute-start.1 = (bf16[3,48,2304]{2,1,0:T(8,128)(2,1)S(1)}, bf16[3,48,2304]{2,1,0:T(8,128)(2,1)S(1)}, u32[]{:S(2)}, u32[]{:S(2)}) collective-permute-start(bf16[3,48,2304]{2,1,0:T(8,128)(2,1)S(1)} %collective-permute-done.refs_0_), channel_id=1, source_target_pairs={{0,2},{1,3},{2,4},{3,5},{4,6},{5,7},{6,8},{7,9},{8,10},{9,11},{10,... | collective-permute-start | bytes 1990664 | tf_op jit(solution)/shard_map/ppermute | solution.py:636
  303.0 15.6 %collective-permute-start.10 = (bf16[3,48,2304]{2,1,0:T(8,128)(2,1)S(1)}, bf16[3,48,2304]{2,1,0:T(8,128)(2,1)S(1)}, u32[]{:S(2)}, u32[]{:S(2)}) collective-permute-start(bf16[3,48,2304]{2,1,0:T(8,128)(2,1)S(1)} %collective-permute-done.9.refs_2_), channel_id=1, source_target_pairs={{0,14},{1,15},{2,0},{3,1},{4,2},{5,3},{6,4},{7,5},{8,6},{9,7},{10,... | collective-permute-start | bytes 1990664 | tf_op jit(solution)/shard_map/ppermute | solution.py:637
  306.4 15.6 %collective-permute-start.2 = (bf16[3,48,2304]{2,1,0:T(8,128)(2,1)S(1)}, bf16[3,48,2304]{2,1,0:T(8,128)(2,1)S(1)}, u32[]{:S(2)}, u32[]{:S(2)}) collective-permute-start(bf16[3,48,2304]{2,1,0:T(8,128)(2,1)S(1)} %collective-permute-done.1.refs_0_), channel_id=1, source_target_pairs={{0,2},{1,3},{2,4},{3,5},{4,6},{5,7},{6,8},{7,9},{8,10},{9,11},{10,... | collective-permute-start | bytes 1990664 | tf_op jit(solution)/shard_map/ppermute | solution.py:636
  306.4 19.7 %collective-permute-start.29 = (bf16[3,48,2304]{2,1,0:T(8,128)(2,1)}, bf16[3,48,2304]{2,1,0:T(8,128)(2,1)S(1)}, u32[]{:S(2)}, u32[]{:S(2)}) collective-permute-start(bf16[3,48,2304]{2,1,0:T(8,128)(2,1)} %get-tuple-element.189.refs_2_), channel_id=1, source_target_pairs={{0,1},{1,0},{2,3},{3,2},{4,5},{5,4},{6,7},{7,6},{8,9},{9,8},{10,11... | collective-permute-start | bytes 1990664 | tf_op jit(solution)/shard_map/ppermute | solution.py:638
  308.8 19.0 %collective-permute-start.28 = (bf16[3,48,2304]{2,1,0:T(8,128)(2,1)}, bf16[3,48,2304]{2,1,0:T(8,128)(2,1)S(1)}, u32[]{:S(2)}, u32[]{:S(2)}) collective-permute-start(bf16[3,48,2304]{2,1,0:T(8,128)(2,1)} %get-tuple-element.187.refs_4_.refs_0_), channel_id=1, source_target_pairs={{0,1},{1,0},{2,3},{3,2},{4,5},{5,4},{6,7},{7,6},{8,9},{9,8},{10,11... | collective-permute-start | bytes 1990664 | tf_op jit(solution)/shard_map/ppermute | solution.py:638
  318.5 14.7 %collective-permute-start.11 = (bf16[3,48,2304]{2,1,0:T(8,128)(2,1)S(1)}, bf16[3,48,2304]{2,1,0:T(8,128)(2,1)S(1)}, u32[]{:S(2)}, u32[]{:S(2)}) collective-permute-start(bf16[3,48,2304]{2,1,0:T(8,128)(2,1)S(1)} %collective-permute-done.10.refs_2_), channel_id=1, source_target_pairs={{0,14},{1,15},{2,0},{3,1},{4,2},{5,3},{6,4},{7,5},{8,6},{9,7},{10,... | collective-permute-start | bytes 1990664 | tf_op jit(solution)/shard_map/ppermute | solution.py:637
  321.9 14.7 %collective-permute-start.3 = (bf16[3,48,2304]{2,1,0:T(8,128)(2,1)S(1)}, bf16[3,48,2304]{2,1,0:T(8,128)(2,1)S(1)}, u32[]{:S(2)}, u32[]{:S(2)}) collective-permute-start(bf16[3,48,2304]{2,1,0:T(8,128)(2,1)S(1)} %collective-permute-done.2.refs_0_), channel_id=1, source_target_pairs={{0,2},{1,3},{2,4},{3,5},{4,6},{5,7},{6,8},{7,9},{8,10},{9,11},{10,... | collective-permute-start | bytes 1990664 | tf_op jit(solution)/shard_map/ppermute | solution.py:636
  322.0 14.7 %collective-permute-start.27 = (bf16[3,48,2304]{2,1,0:T(8,128)(2,1)S(1)}, bf16[3,48,2304]{2,1,0:T(8,128)(2,1)S(1)}, u32[]{:S(2)}, u32[]{:S(2)}) collective-permute-start(bf16[3,48,2304]{2,1,0:T(8,128)(2,1)S(1)} %collective-permute-done.8.refs_2_), channel_id=1, source_target_pairs={{0,1},{1,0},{2,3},{3,2},{4,5},{5,4},{6,7},{7,6},{8,9},{9,8},{10,11... | collective-permute-start | bytes 1990664 | tf_op jit(solution)/shard_map/ppermute | solution.py:638
  326.9 14.8 %collective-permute-start.26 = (bf16[3,48,2304]{2,1,0:T(8,128)(2,1)S(1)}, bf16[3,48,2304]{2,1,0:T(8,128)(2,1)S(1)}, u32[]{:S(2)}, u32[]{:S(2)}) collective-permute-start(bf16[3,48,2304]{2,1,0:T(8,128)(2,1)S(1)} %collective-permute-done.refs_0_), channel_id=1, source_target_pairs={{0,1},{1,0},{2,3},{3,2},{4,5},{5,4},{6,7},{7,6},{8,9},{9,8},{10,11... | collective-permute-start | bytes 1990664 | tf_op jit(solution)/shard_map/ppermute | solution.py:638
  328.6 14.8 %collective-permute-start.25 = (bf16[3,48,2304]{2,1,0:T(8,128)(2,1)S(1)}, bf16[3,48,2304]{2,1,0:T(8,128)(2,1)S(1)}, u32[]{:S(2)}, u32[]{:S(2)}) collective-permute-start(bf16[3,48,2304]{2,1,0:T(8,128)(2,1)S(1)} %collective-permute-done.9.refs_2_), channel_id=1, source_target_pairs={{0,1},{1,0},{2,3},{3,2},{4,5},{5,4},{6,7},{7,6},{8,9},{9,8},{10,11... | collective-permute-start | bytes 1990664 | tf_op jit(solution)/shard_map/ppermute | solution.py:638
  333.2 13.9 %collective-permute-start.12 = (bf16[3,48,2304]{2,1,0:T(8,128)(2,1)S(1)}, bf16[3,48,2304]{2,1,0:T(8,128)(2,1)S(1)}, u32[]{:S(2)}, u32[]{:S(2)}) collective-permute-start(bf16[3,48,2304]{2,1,0:T(8,128)(2,1)S(1)} %collective-permute-done.11.refs_2_), channel_id=1, source_target_pairs={{0,14},{1,15},{2,0},{3,1},{4,2},{5,3},{6,4},{7,5},{8,6},{9,7},{10,... | collective-permute-start | bytes 1990664 | tf_op jit(solution)/shard_map/ppermute | solution.py:637
  336.7 13.9 %collective-permute-start.4 = (bf16[3,48,2304]{2,1,0:T(8,128)(2,1)S(1)}, bf16[3,48,2304]{2,1,0:T(8,128)(2,1)}, u32[]{:S(2)}, u32[]{:S(2)}) collective-permute-start(bf16[3,48,2304]{2,1,0:T(8,128)(2,1)S(1)} %collective-permute-done.3.refs_0_), channel_id=1, source_target_pairs={{0,2},{1,3},{2,4},{3,5},{4,6},{5,7},{6,8},{7,9},{8,10},{9,11},{10,... | collective-permute-start | bytes 1990664 | tf_op jit(solution)/shard_map/ppermute | solution.py:636
  337.5 13.0 %collective-permute-start.24 = (bf16[3,48,2304]{2,1,0:T(8,128)(2,1)S(1)}, bf16[3,48,2304]{2,1,0:T(8,128)(2,1)S(1)}, u32[]{:S(2)}, u32[]{:S(2)}) collective-permute-start(bf16[3,48,2304]{2,1,0:T(8,128)(2,1)S(1)} %collective-permute-done.1.refs_0_), channel_id=1, source_target_pairs={{0,1},{1,0},{2,3},{3,2},{4,5},{5,4},{6,7},{7,6},{8,9},{9,8},{10,11... | collective-permute-start | bytes 1990664 | tf_op jit(solution)/shard_map/ppermute | solution.py:638
  342.5 14.4 %collective-permute-start.23 = (bf16[3,48,2304]{2,1,0:T(8,128)(2,1)S(1)}, bf16[3,48,2304]{2,1,0:T(8,128)(2,1)S(1)}, u32[]{:S(2)}, u32[]{:S(2)}) collective-permute-start(bf16[3,48,2304]{2,1,0:T(8,128)(2,1)S(1)} %collective-permute-done.10.refs_2_), channel_id=1, source_target_pairs={{0,1},{1,0},{2,3},{3,2},{4,5},{5,4},{6,7},{7,6},{8,9},{9,8},{10,11... | collective-permute-start | bytes 1990664 | tf_op jit(solution)/shard_map/ppermute | solution.py:638
  344.2 13.6 %collective-permute-start.22 = (bf16[3,48,2304]{2,1,0:T(8,128)(2,1)S(1)}, bf16[3,48,2304]{2,1,0:T(8,128)(2,1)S(1)}, u32[]{:S(2)}, u32[]{:S(2)}) collective-permute-start(bf16[3,48,2304]{2,1,0:T(8,128)(2,1)S(1)} %collective-permute-done.2.refs_0_), channel_id=1, source_target_pairs={{0,1},{1,0},{2,3},{3,2},{4,5},{5,4},{6,7},{7,6},{8,9},{9,8},{10,11... | collective-permute-start | bytes 1990664 | tf_op jit(solution)/shard_map/ppermute | solution.py:638
  347.1 13.4 %collective-permute-start.13 = (bf16[3,48,2304]{2,1,0:T(8,128)(2,1)S(1)}, bf16[3,48,2304]{2,1,0:T(8,128)(2,1)}, u32[]{:S(2)}, u32[]{:S(2)}) collective-permute-start(bf16[3,48,2304]{2,1,0:T(8,128)(2,1)S(1)} %collective-permute-done.12.refs_2_), channel_id=1, source_target_pairs={{0,14},{1,15},{2,0},{3,1},{4,2},{5,3},{6,4},{7,5},{8,6},{9,7},{10,... | collective-permute-start | bytes 1990664 | tf_op jit(solution)/shard_map/ppermute | solution.py:637
  350.5 13.5 %collective-permute-start.5 = (bf16[3,48,2304]{2,1,0:T(8,128)(2,1)}, bf16[3,48,2304]{2,1,0:T(8,128)(2,1)}, u32[]{:S(2)}, u32[]{:S(2)}) collective-permute-start(bf16[3,48,2304]{2,1,0:T(8,128)(2,1)} %collective-permute-done.4.refs_0_), channel_id=1, source_target_pairs={{0,2},{1,3},{2,4},{3,5},{4,6},{5,7},{6,8},{7,9},{8,10},{9,11},{10,... | collective-permute-start | bytes 1990664 | tf_op jit(solution)/shard_map/ppermute | solution.py:636
  351.4 15.0 %collective-permute-start.21 = (bf16[3,48,2304]{2,1,0:T(8,128)(2,1)S(1)}, bf16[3,48,2304]{2,1,0:T(8,128)(2,1)}, u32[]{:S(2)}, u32[]{:S(2)}) collective-permute-start(bf16[3,48,2304]{2,1,0:T(8,128)(2,1)S(1)} %collective-permute-done.11.refs_2_), channel_id=1, source_target_pairs={{0,1},{1,0},{2,3},{3,2},{4,5},{5,4},{6,7},{7,6},{8,9},{9,8},{10,11... | collective-permute-start | bytes 1990664 | tf_op jit(solution)/shard_map/ppermute | solution.py:638
  357.8 15.4 %collective-permute-start.20 = (bf16[3,48,2304]{2,1,0:T(8,128)(2,1)S(1)}, bf16[3,48,2304]{2,1,0:T(8,128)(2,1)}, u32[]{:S(2)}, u32[]{:S(2)}) collective-permute-start(bf16[3,48,2304]{2,1,0:T(8,128)(2,1)S(1)} %collective-permute-done.3.refs_0_), channel_id=1, source_target_pairs={{0,1},{1,0},{2,3},{3,2},{4,5},{5,4},{6,7},{7,6},{8,9},{9,8},{10,11... | collective-permute-start | bytes 1990664 | tf_op jit(solution)/shard_map/ppermute | solution.py:638
  358.7 14.7 %collective-permute-start.19 = (bf16[3,48,2304]{2,1,0:T(8,128)(2,1)S(1)}, bf16[3,48,2304]{2,1,0:T(8,128)(2,1)}, u32[]{:S(2)}, u32[]{:S(2)}) collective-permute-start(bf16[3,48,2304]{2,1,0:T(8,128)(2,1)S(1)} %collective-permute-done.12.refs_2_), channel_id=1, source_target_pairs={{0,1},{1,0},{2,3},{3,2},{4,5},{5,4},{6,7},{7,6},{8,9},{9,8},{10,11... | collective-permute-start | bytes 1990664 | tf_op jit(solution)/shard_map/ppermute | solution.py:638
  360.5 13.5 %collective-permute-start.14 = (bf16[3,48,2304]{2,1,0:T(8,128)(2,1)}, bf16[3,48,2304]{2,1,0:T(8,128)(2,1)}, u32[]{:S(2)}, u32[]{:S(2)}) collective-permute-start(bf16[3,48,2304]{2,1,0:T(8,128)(2,1)} %collective-permute-done.13.refs_2_), channel_id=1, source_target_pairs={{0,14},{1,15},{2,0},{3,1},{4,2},{5,3},{6,4},{7,5},{8,6},{9,7},{10,... | collective-permute-start | bytes 1990664 | tf_op jit(solution)/shard_map/ppermute | solution.py:637
  364.0 16.3 %collective-permute-start.6 = (bf16[3,48,2304]{2,1,0:T(8,128)(2,1)}, bf16[3,48,2304]{2,1,0:T(8,128)(2,1)}, u32[]{:S(2)}, u32[]{:S(2)}) collective-permute-start(bf16[3,48,2304]{2,1,0:T(8,128)(2,1)} %collective-permute-done.5.refs_0_), channel_id=1, source_target_pairs={{0,2},{1,3},{2,4},{3,5},{4,6},{5,7},{6,8},{7,9},{8,10},{9,11},{10,... | collective-permute-start | bytes 1990664 | tf_op jit(solution)/shard_map/ppermute | solution.py:636
  366.4 81.8 %collective-permute-start.18 = (bf16[3,48,2304]{2,1,0:T(8,128)(2,1)}, bf16[3,48,2304]{2,1,0:T(8,128)(2,1)}, u32[]{:S(2)}, u32[]{:S(2)}) collective-permute-start(bf16[3,48,2304]{2,1,0:T(8,128)(2,1)} %collective-permute-done.4.refs_0_), channel_id=1, source_target_pairs={{0,1},{1,0},{2,3},{3,2},{4,5},{5,4},{6,7},{7,6},{8,9},{9,8},{10,11... | collective-permute-start | bytes 1990664 | tf_op jit(solution)/shard_map/ppermute | solution.py:638
  373.2 87.5 %collective-permute-start.17 = (bf16[3,48,2304]{2,1,0:T(8,128)(2,1)}, bf16[3,48,2304]{2,1,0:T(8,128)(2,1)}, u32[]{:S(2)}, u32[]{:S(2)}) collective-permute-start(bf16[3,48,2304]{2,1,0:T(8,128)(2,1)} %collective-permute-done.13.refs_2_), channel_id=1, source_target_pairs={{0,1},{1,0},{2,3},{3,2},{4,5},{5,4},{6,7},{7,6},{8,9},{9,8},{10,11... | collective-permute-start | bytes 1990664 | tf_op jit(solution)/shard_map/ppermute | solution.py:638
  373.4 87.4 %collective-permute-start.16 = (bf16[3,48,2304]{2,1,0:T(8,128)(2,1)}, bf16[3,48,2304]{2,1,0:T(8,128)(2,1)}, u32[]{:S(2)}, u32[]{:S(2)}) collective-permute-start(bf16[3,48,2304]{2,1,0:T(8,128)(2,1)} %collective-permute-done.5.refs_0_), channel_id=1, source_target_pairs={{0,1},{1,0},{2,3},{3,2},{4,5},{5,4},{6,7},{7,6},{8,9},{9,8},{10,11... | collective-permute-start | bytes 1990664 | tf_op jit(solution)/shard_map/ppermute | solution.py:638
  373.9 99.5 %collective-permute-start.15 = (bf16[3,48,2304]{2,1,0:T(8,128)(2,1)}, bf16[3,48,2304]{2,1,0:T(8,128)(2,1)}, u32[]{:S(2)}, u32[]{:S(2)}) collective-permute-start(bf16[3,48,2304]{2,1,0:T(8,128)(2,1)} %collective-permute-done.14.refs_2_), channel_id=1, source_target_pairs={{0,1},{1,0},{2,3},{3,2},{4,5},{5,4},{6,7},{7,6},{8,9},{9,8},{10,11... | collective-permute-start | bytes 1990664 | tf_op jit(solution)/shard_map/ppermute | solution.py:638
  380.3 93.1 %collective-permute-start.7 = (bf16[3,48,2304]{2,1,0:T(8,128)(2,1)}, bf16[3,48,2304]{2,1,0:T(8,128)(2,1)}, u32[]{:S(2)}, u32[]{:S(2)}) collective-permute-start(bf16[3,48,2304]{2,1,0:T(8,128)(2,1)} %collective-permute-done.6.refs_0_), channel_id=1, source_target_pairs={{0,1},{1,0},{2,3},{3,2},{4,5},{5,4},{6,7},{7,6},{8,9},{9,8},{10,11... | collective-permute-start | bytes 1990664 | tf_op jit(solution)/shard_map/ppermute | solution.py:638
  (26 other events, 132.5 us)

commit v2 on v1

--- a/solution.py
+++ b/solution.py
@@ -67,7 +67,7 @@
     return pl.BlockSpec((1, block, d), lambda i, k: (number, k, 0))
 
 
-def forward_up(number, h, w_gate, w_up, tall=1024, block=768):
+def forward_up(number, h, w_gate, w_up, tall=512, block=768):
     tokens, d = h.shape
     ff = w_gate.shape[2]
     rows = pl.BlockSpec((tall, d), lambda i, k: (i, 0))
@@ -114,7 +114,7 @@
     all_ref[2], all_ref[0], all_ref[1] = gated_back(wide_dot(a, gate_ref[0]), wide_dot(a, up_ref[0]), by_mid)
 
 
-def last_layer(number, h, by, w_gate, w_up, w_down, tall=1024, block=768):
+def last_layer(number, h, by, w_gate, w_up, w_down, tall=512, block=768):
     tokens, d = h.shape
     ff = w_gate.shape[2]
     rows = pl.BlockSpec((tall, d), lambda i, k: (i, 0))
@@ -134,8 +134,13 @@
 
 
 def turn(a_ref, by_ref, turned):
-    turned[0] = a_ref[...].T
-    turned[1] = by_ref[...].T
+    deep = 256
+
+    @pl.loop(0, a_ref.shape[0] // deep)
+    def _(k):
+        at = pl.ds(pl.multiple_of(k * deep, deep), deep)
+        turned[0, :, at] = a_ref[at, :].T
+        turned[1, :, at] = by_ref[at, :].T
 
 
 def part_specs(tokens, d, ff, block):
@@ -343,13 +348,14 @@
 
 
 def squares_of(ref):
-    squares = jnp.zeros((8, 128), F32)
-    for i in range(ref.shape[0]):
+    def more(i, squares):
         value = ref[i].astype(F32)
         flat = jnp.sum((value * value).reshape(-1, 8, value.shape[1]), axis=0)
         for k in range(flat.shape[1] // 128):
             squares = squares + flat[:, 128 * k : 128 * (k + 1)]
-    return squares
+        return squares
+
+    return lax.fori_loop(0, ref.shape[0], more, jnp.zeros((8, 128), F32))
 
 
 def weight_ring_kernel(n, *refs):
@@ -562,7 +568,9 @@
 
         @pl.when(part == p)
         def _():
-            g_ref[...] = pieces[p][...]
+            @pl.loop(0, g_ref.shape[0])
+            def _(k):
+                g_ref[k] = pieces[p][k]
 
     factor = factor_ref[0]
     for which in range(3):

time: 495 us -> 496 us (level); the launches traced: 486 us -> 496 us
  Pallas kernels: 367 us -> 377 us
where the time goes in v2:
time: 496 us
  Pallas kernels  377 us (76%)
  starting transfers between devices  55.3 us (11%)
  waiting for transfers between devices  44.9 us (9%)
  local copies, waits for them, and re-layouts  14.9 us (3%)
    pallas_call x1, Pallas kernels, weights_summed(): pl.pallas_call(functools.partial(weight_ring_kernel, n), out_shape=(jax.S...  97.4 us
    pallas_call x8, Pallas kernels, adam(): pl.pallas_call(functools.partial(adam_kernel, first), out_shape=shapes, g...  97.3 us
    pallas_call x1, Pallas kernels, first_layer(): pl.pallas_call(functools.partial(first_kernel, n, block), out_shape=(jax....  74.4 us
    ppermute x7, waiting for transfers between devices, step(): left = lax.ppermute(left, 'dp', behind)  44.8 us
    pallas_call x1, Pallas kernels, last_layer(): pl.pallas_call(last_kernel, out_shape=(jax.ShapeDtypeStruct((tokens, d),...  36.9 us
    pallas_call x1, Pallas kernels, by_weights(): pl.pallas_call(weight_kernel, out_shape=(jax.ShapeDtypeStruct((2, d, ff),...  33.3 us
    pallas_call x1, Pallas kernels, forward_up(): pl.pallas_call(up_kernel, out_shape=(jax.ShapeDtypeStruct((tokens, d), BF...  24.7 us
    ppermute x7, starting transfers between devices, step(): left = lax.ppermute(left, 'dp', behind)  21.4 us
  transfers between devices with their start and end apart: 30, of which 7 were waited for; matrix products, arithmetic and copies ran while one was open for 0% of the time, Pallas kernels for 17%

profile of v2, /device:TPU:21, one launch (start us, length us, event | category | flops | bytes accessed | tf_op | source)
XLA Modules:
  0.0 495.6 jit_solution(15998404668672373938)
XLA Ops:
  0.6 24.7 %forward_up.1 = (bf16[2048,768]{1,0:T(8,128)(2,1)}, bf16[2048,2304]{1,0:T(8,128)(2,1)}) custom-call(bf16[2048,768]{1,0:T(8,128)(2,1)} %bitcast.39, bf16[2,768,2304]{2,1,0:T(8,128)(2,1)} %refs_4_.17, bf16[2,768,2304]{2,1,0:T(8,128)(2,1)} %refs_5_.15), custom_call_target="tpu_custom_call" | custom-call | flops 14495514624 | bytes 27262976 | tf_op jit(solution)/shard_map/forward_up/pallas_call | solution.py:75
  25.3 12.7 %forward_down.1.h_ref.refs_6_ = bf16[2048,768]{1,0:T(8,128)(2,1)} custom-call(bf16[2048,2304]{1,0:T(8,128)(2,1)} %get-tuple-element.180.mid_ref.refs_2_, bf16[2,2304,768]{2,1,0:T(8,128)(2,1)} %refs_6_.15, bf16[2048,768]{1,0:T(8,128)(2,1)} %bitcast.40), custom_call_target="tpu_custom_call" | custom-call | flops 7247757312 | bytes 20971520 | tf_op jit(solution)/shard_map/forward_down/pallas_call | solution.py:95
  38.0 36.9 %last_layer.1 = (bf16[2048,768]{1,0:T(8,128)(2,1)}, bf16[3,2048,2304]{2,1,0:T(8,128)(2,1)}) custom-call(bf16[2048,768]{1,0:T(8,128)(2,1)} %forward_down.1.h_ref.refs_6_, bf16[2048,768]{1,0:T(8,128)(2,1)} %bitcast.41, bf16[2,768,2304]{2,1,0:T(8,128)(2,1)} %refs_4_.17, bf16[2,768,2304]{2,1,0:T(8,128)(2,1)} %refs_5_.15, bf16[2,2304,768]{2,1,0:T(8,128)(2,1)} %refs_6_.15), custom_call_target="tpu_custom_call" | custom-call | flops 21743271936 | bytes 62914560 | tf_op jit(solution)/shard_map/last_layer/pallas_call | solution.py:121
  74.9 33.3 %by_weights.1 = (bf16[2,768,2304]{2,1,0:T(8,128)(2,1)}, bf16[2304,768]{1,0:T(8,128)(2,1)}) custom-call(bf16[2048,768]{1,0:T(8,128)(2,1)} %get-tuple-element.181.a_ref, bf16[2048,768]{1,0:T(8,128)(2,1)} %bitcast.42, bf16[3,2048,2304]{2,1,0:T(8,128)(2,1)} %get-tuple-element.182.all_ref.refs_5_), custom_call_target="tpu_custom_call" | custom-call | flops 21743271936 | bytes 47185920 | tf_op jit(solution)/shard_map/by_weights/pallas_call | solution.py:179
  108.2 74.4 %first_layer.1 = (bf16[3,48,2304]{2,1,0:T(8,128)(2,1)}, bf16[2048,768]{1,0:T(8,128)(2,1)}, bf16[2,2048,2304]{2,1,0:T(8,128)(2,1)}) custom-call(bf16[2,8,2,48,2304]{4,3,2,1,0:T(8,128)(2,1)} %bitcast.44, bf16[8,2,3,48,768]{4,3,2,1,0:T(8,128)(2,1)} %bitcast.45, bf16[2,768,2304]{2,1,0:T(8,128)(2,1)} %refs_4_.17, bf16[2,768,2304]{2,1,0:T(8,128)(2,1)} %refs_5_.15, ...), custom_call_target="tpu_custom_call" | custom-call | flops 36238786560 | bytes 62914560 | tf_op jit(solution)/shard_map/first_layer/pallas_call | solution.py:539
  182.6 97.4 %weights_summed.1 = (bf16[3,48,2304]{2,1,0:T(8,128)(2,1)}, f32[8,128]{1,0:T(8,128)}) custom-call(bf16[2048,768]{1,0:T(8,128)(2,1)} %get-tuple-element.179.refs_8_.refs_0_, bf16[2048,768]{1,0:T(8,128)(2,1)} %get-tuple-element.185.refs_1_, bf16[2048,2304]{1,0:T(8,128)(2,1)} %get-tuple-element.180.mid_ref.refs_2_, ...), custom_call_target="tpu_custom_call" | custom-call | flops 21743271936 | bytes 47185920 | tf_op jit(solution)/shard_map/weights_summed/pallas_call | solution.py:449
  280.0 1.6 collective-permute-start.8
  281.6 14.8 %collective-permute-done.8.refs_2_ = bf16[3,48,2304]{2,1,0:T(8,128)(2,1)S(1)} collective-permute-done((bf16[3,48,2304]{2,1,0:T(8,128)(2,1)}, bf16[3,48,2304]{2,1,0:T(8,128)(2,1)S(1)}, u32[]{:S(2)}, u32[]{:S(2)}) %collective-permute-start.8) | collective-permute-done | bytes 663584 | tf_op jit(solution)/shard_map/ppermute | solution.py:645
  296.4 2.7 collective-permute-start.9
  299.0 13.0 %collective-permute-done.9.refs_2_ = bf16[3,48,2304]{2,1,0:T(8,128)(2,1)S(1)} collective-permute-done((bf16[3,48,2304]{2,1,0:T(8,128)(2,1)S(1)}, bf16[3,48,2304]{2,1,0:T(8,128)(2,1)S(1)}, u32[]{:S(2)}, u32[]{:S(2)}) %collective-permute-start.9) | collective-permute-done | bytes 663584 | tf_op jit(solution)/shard_map/ppermute | solution.py:645
  312.0 3.4 collective-permute-start.10
  315.5 2.4 collective-permute-start.29
  318.0 9.6 %collective-permute-done.10.refs_2_ = bf16[3,48,2304]{2,1,0:T(8,128)(2,1)S(1)} collective-permute-done((bf16[3,48,2304]{2,1,0:T(8,128)(2,1)S(1)}, bf16[3,48,2304]{2,1,0:T(8,128)(2,1)S(1)}, u32[]{:S(2)}, u32[]{:S(2)}) %collective-permute-start.10) | collective-permute-done | bytes 663584 | tf_op jit(solution)/shard_map/ppermute | solution.py:645
  327.6 3.4 collective-permute-start.11
  331.0 3.2 collective-permute-start.27
  338.2 4.2 collective-permute-done.11.refs_2_
  342.3 3.4 collective-permute-start.12
  346.6 4.1 collective-permute-start.24
  356.2 3.4 collective-permute-start.13
  360.5 5.3 %collective-permute-start.21 = (bf16[3,48,2304]{2,1,0:T(8,128)(2,1)S(1)}, bf16[3,48,2304]{2,1,0:T(8,128)(2,1)}, u32[]{:S(2)}, u32[]{:S(2)}) collective-permute-start(bf16[3,48,2304]{2,1,0:T(8,128)(2,1)S(1)} %collective-permute-done.11.refs_2_), channel_id=1, source_target_pairs={{0,1},{1,0},{2,3},{3,2},{4,5},{5,4},{6,7},{7,6},{8,9},{9,8},{10,11... | collective-permute-start | bytes 1990664 | tf_op jit(solution)/shard_map/ppermute | solution.py:646
  369.5 3.5 collective-permute-start.14
  375.5 6.8 %collective-permute-start.18 = (bf16[3,48,2304]{2,1,0:T(8,128)(2,1)}, bf16[3,48,2304]{2,1,0:T(8,128)(2,1)}, u32[]{:S(2)}, u32[]{:S(2)}) collective-permute-start(bf16[3,48,2304]{2,1,0:T(8,128)(2,1)} %collective-permute-done.4.refs_0_), channel_id=1, source_target_pairs={{0,1},{1,0},{2,3},{3,2},{4,5},{5,4},{6,7},{7,6},{8,9},{9,8},{10,11... | collective-permute-start | bytes 1990664 | tf_op jit(solution)/shard_map/ppermute | solution.py:646
  383.0 6.4 %collective-permute-start.15 = (bf16[3,48,2304]{2,1,0:T(8,128)(2,1)}, bf16[3,48,2304]{2,1,0:T(8,128)(2,1)}, u32[]{:S(2)}, u32[]{:S(2)}) collective-permute-start(bf16[3,48,2304]{2,1,0:T(8,128)(2,1)} %collective-permute-done.14.refs_2_), channel_id=1, source_target_pairs={{0,1},{1,0},{2,3},{3,2},{4,5},{5,4},{6,7},{7,6},{8,9},{9,8},{10,11... | collective-permute-start | bytes 1990664 | tf_op jit(solution)/shard_map/ppermute | solution.py:646
  389.4 3.4 collective-permute-start.7
  397.9 11.8 %adam_step.8 = (bf16[2,768,2304]{2,1,0:T(8,128)(2,1)}, bf16[2,768,2304]{2,1,0:T(8,128)(2,1)}, bf16[2,2304,768]{2,1,0:T(8,128)(2,1)}, f32[2,768,2304]{2,1,0:T(8,1...) custom-call(s32[2,4]{1,0:T(2,128)S(1)} %scatter.39.where_ref, ...), custom_call_target="tpu_custom_call" | custom-call | flops 60000000 | bytes 29196288 | tf_op jit(solution)/shard_map/adam_step/pallas_call | solution.py:602
  409.7 11.8 %adam_step.9 = (bf16[2,768,2304]{2,1,0:T(8,128)(2,1)}, bf16[2,768,2304]{2,1,0:T(8,128)(2,1)}, bf16[2,2304,768]{2,1,0:T(8,128)(2,1)}, f32[2,768,2304]{2,1,0:T(8,1...) custom-call(s32[2,4]{1,0:T(2,128)S(1)} %scatter.36.where_ref, ...), custom_call_target="tpu_custom_call", output_to_operand_aliasing={{0}: (15, {}), {1}: (16, {}), {2}: (17, {}), {3}: (18, {}),... | custom-call | flops 60000000 | bytes 29196288 | tf_op jit(solution)/shard_map/adam_step/pallas_call | solution.py:602
  421.6 11.8 %adam_step.10 = (bf16[2,768,2304]{2,1,0:T(8,128)(2,1)}, bf16[2,768,2304]{2,1,0:T(8,128)(2,1)}, bf16[2,2304,768]{2,1,0:T(8,128)(2,1)}, f32[2,768,2304]{2,1,0:T(8,...) custom-call(s32[2,4]{1,0:T(2,128)S(1)} %scatter.35.where_ref, ...), custom_call_target="tpu_custom_call", output_to_operand_aliasing={{0}: (15, {}), {1}: (16, {}), {2}: (17, {}), {3}: (18, {}),... | custom-call | flops 60000000 | bytes 29196288 | tf_op jit(solution)/shard_map/adam_step/pallas_call | solution.py:602
  433.4 11.8 %adam_step.11 = (bf16[2,768,2304]{2,1,0:T(8,128)(2,1)}, bf16[2,768,2304]{2,1,0:T(8,128)(2,1)}, bf16[2,2304,768]{2,1,0:T(8,128)(2,1)}, f32[2,768,2304]{2,1,0:T(8,...) custom-call(s32[2,4]{1,0:T(2,128)S(1)} %scatter.34.where_ref, ...), custom_call_target="tpu_custom_call", output_to_operand_aliasing={{0}: (15, {}), {1}: (16, {}), {2}: (17, {}), {3}: (18, {}),... | custom-call | flops 60000000 | bytes 29196288 | tf_op jit(solution)/shard_map/adam_step/pallas_call | solution.py:602
  445.2 12.3 %adam_step.12 = (bf16[2,768,2304]{2,1,0:T(8,128)(2,1)}, bf16[2,768,2304]{2,1,0:T(8,128)(2,1)}, bf16[2,2304,768]{2,1,0:T(8,128)(2,1)}, f32[2,768,2304]{2,1,0:T(8,...) custom-call(s32[2,4]{1,0:T(2,128)S(1)} %scatter.31.where_ref, ...), custom_call_target="tpu_custom_call", output_to_operand_aliasing={{0}: (15, {}), {1}: (16, {}), {2}: (17, {}), {3}: (18, {}),... | custom-call | flops 60000000 | bytes 29196288 | tf_op jit(solution)/shard_map/adam_step/pallas_call | solution.py:602
  457.5 12.5 %adam_step.13 = (bf16[2,768,2304]{2,1,0:T(8,128)(2,1)}, bf16[2,768,2304]{2,1,0:T(8,128)(2,1)}, bf16[2,2304,768]{2,1,0:T(8,128)(2,1)}, f32[2,768,2304]{2,1,0:T(8,...) custom-call(s32[2,4]{1,0:T(2,128)S(1)} %scatter.30.where_ref, ...), custom_call_target="tpu_custom_call", output_to_operand_aliasing={{0}: (15, {}), {1}: (16, {}), {2}: (17, {}), {3}: (18, {}),... | custom-call | flops 60000000 | bytes 29196288 | tf_op jit(solution)/shard_map/adam_step/pallas_call | solution.py:602
  470.0 12.7 %adam_step.14 = (bf16[2,768,2304]{2,1,0:T(8,128)(2,1)}, bf16[2,768,2304]{2,1,0:T(8,128)(2,1)}, bf16[2,2304,768]{2,1,0:T(8,128)(2,1)}, f32[2,768,2304]{2,1,0:T(8,...) custom-call(s32[2,4]{1,0:T(2,128)S(1)} %scatter.29.where_ref, ...), custom_call_target="tpu_custom_call", output_to_operand_aliasing={{0}: (15, {}), {1}: (16, {}), {2}: (17, {}), {3}: (18, {}),... | custom-call | flops 60000000 | bytes 29196288 | tf_op jit(solution)/shard_map/adam_step/pallas_call | solution.py:602
  482.7 12.7 %adam_step.15 = (bf16[2,768,2304]{2,1,0:T(8,128)(2,1)}, bf16[2,768,2304]{2,1,0:T(8,128)(2,1)}, bf16[2,2304,768]{2,1,0:T(8,128)(2,1)}, f32[2,768,2304]{2,1,0:T(8,...) custom-call(s32[2,4]{1,0:T(2,128)S(1)} %scatter.26.where_ref, ...), custom_call_target="tpu_custom_call", output_to_operand_aliasing={{0}: (15, {}), {1}: (16, {}), {2}: (17, {}), {3}: (18, {}),... | custom-call | flops 60000000 | bytes 29196288 | tf_op jit(solution)/shard_map/adam_step/pallas_call | solution.py:602
  (123 shorter events, 22.3 us)
Async XLA Ops:
  182.6 99.0 %copy-start.4 = (bf16[3,48,2304]{2,1,0:T(8,128)(2,1)S(1)}, bf16[3,48,2304]{2,1,0:T(8,128)(2,1)}, u32[]{:S(2)}) copy-start(bf16[3,48,2304]{2,1,0:T(8,128)(2,1)} %get-tuple-element.187.refs_4_.refs_0_) | copy-start | bytes 1990660
  182.6 190.5 %copy-start.27 = (s32[2,4]{1,0:T(2,128)S(1)}, s32[2,4]{1,0:T(2,128)}, u32[]{:S(2)}) copy-start(s32[2,4]{1,0:T(2,128)} %constant.302.clone) | copy-start | bytes 100
  280.0 16.4 %collective-permute-start.8 = (bf16[3,48,2304]{2,1,0:T(8,128)(2,1)}, bf16[3,48,2304]{2,1,0:T(8,128)(2,1)S(1)}, u32[]{:S(2)}, u32[]{:S(2)}) collective-permute-start(bf16[3,48,2304]{2,1,0:T(8,128)(2,1)} %get-tuple-element.189.refs_2_), channel_id=1, source_target_pairs={{0,14},{1,15},{2,0},{3,1},{4,2},{5,3},{6,4},{7,5},{8,6},{9,7},{10,... | collective-permute-start | bytes 1990664 | tf_op jit(solution)/shard_map/ppermute | solution.py:645
  281.5 17.5 %collective-permute-start = (bf16[3,48,2304]{2,1,0:T(8,128)(2,1)S(1)}, bf16[3,48,2304]{2,1,0:T(8,128)(2,1)S(1)}, u32[]{:S(2)}, u32[]{:S(2)}) collective-permute-start(bf16[3,48,2304]{2,1,0:T(8,128)(2,1)S(1)} %copy-done.4), channel_id=1, source_target_pairs={{0,2},{1,3},{2,4},{3,5},{4,6},{5,7},{6,8},{7,9},{8,10},{9,11},{10,... | collective-permute-start | bytes 1990664 | tf_op jit(solution)/shard_map/ppermute | solution.py:644
  296.4 15.7 %collective-permute-start.9 = (bf16[3,48,2304]{2,1,0:T(8,128)(2,1)S(1)}, bf16[3,48,2304]{2,1,0:T(8,128)(2,1)S(1)}, u32[]{:S(2)}, u32[]{:S(2)}) collective-permute-start(bf16[3,48,2304]{2,1,0:T(8,128)(2,1)S(1)} %collective-permute-done.8.refs_2_), channel_id=1, source_target_pairs={{0,14},{1,15},{2,0},{3,1},{4,2},{5,3},{6,4},{7,5},{8,6},{9,7},{10,... | collective-permute-start | bytes 1990664 | tf_op jit(solution)/shard_map/ppermute | solution.py:645
  299.0 16.4 %collective-permute-start.1 = (bf16[3,48,2304]{2,1,0:T(8,128)(2,1)S(1)}, bf16[3,48,2304]{2,1,0:T(8,128)(2,1)S(1)}, u32[]{:S(2)}, u32[]{:S(2)}) collective-permute-start(bf16[3,48,2304]{2,1,0:T(8,128)(2,1)S(1)} %collective-permute-done.refs_0_), channel_id=1, source_target_pairs={{0,2},{1,3},{2,4},{3,5},{4,6},{5,7},{6,8},{7,9},{8,10},{9,11},{10,... | collective-permute-start | bytes 1990664 | tf_op jit(solution)/shard_map/ppermute | solution.py:644
  312.0 15.6 %collective-permute-start.10 = (bf16[3,48,2304]{2,1,0:T(8,128)(2,1)S(1)}, bf16[3,48,2304]{2,1,0:T(8,128)(2,1)S(1)}, u32[]{:S(2)}, u32[]{:S(2)}) collective-permute-start(bf16[3,48,2304]{2,1,0:T(8,128)(2,1)S(1)} %collective-permute-done.9.refs_2_), channel_id=1, source_target_pairs={{0,14},{1,15},{2,0},{3,1},{4,2},{5,3},{6,4},{7,5},{8,6},{9,7},{10,... | collective-permute-start | bytes 1990664 | tf_op jit(solution)/shard_map/ppermute | solution.py:645
  315.5 15.6 %collective-permute-start.2 = (bf16[3,48,2304]{2,1,0:T(8,128)(2,1)S(1)}, bf16[3,48,2304]{2,1,0:T(8,128)(2,1)S(1)}, u32[]{:S(2)}, u32[]{:S(2)}) collective-permute-start(bf16[3,48,2304]{2,1,0:T(8,128)(2,1)S(1)} %collective-permute-done.1.refs_0_), channel_id=1, source_target_pairs={{0,2},{1,3},{2,4},{3,5},{4,6},{5,7},{6,8},{7,9},{8,10},{9,11},{10,... | collective-permute-start | bytes 1990664 | tf_op jit(solution)/shard_map/ppermute | solution.py:644
  315.5 19.7 %collective-permute-start.29 = (bf16[3,48,2304]{2,1,0:T(8,128)(2,1)}, bf16[3,48,2304]{2,1,0:T(8,128)(2,1)S(1)}, u32[]{:S(2)}, u32[]{:S(2)}) collective-permute-start(bf16[3,48,2304]{2,1,0:T(8,128)(2,1)} %get-tuple-element.189.refs_2_), channel_id=1, source_target_pairs={{0,1},{1,0},{2,3},{3,2},{4,5},{5,4},{6,7},{7,6},{8,9},{9,8},{10,11... | collective-permute-start | bytes 1990664 | tf_op jit(solution)/shard_map/ppermute | solution.py:646
  317.9 19.0 %collective-permute-start.28 = (bf16[3,48,2304]{2,1,0:T(8,128)(2,1)}, bf16[3,48,2304]{2,1,0:T(8,128)(2,1)S(1)}, u32[]{:S(2)}, u32[]{:S(2)}) collective-permute-start(bf16[3,48,2304]{2,1,0:T(8,128)(2,1)} %get-tuple-element.187.refs_4_.refs_0_), channel_id=1, source_target_pairs={{0,1},{1,0},{2,3},{3,2},{4,5},{5,4},{6,7},{7,6},{8,9},{9,8},{10,11... | collective-permute-start | bytes 1990664 | tf_op jit(solution)/shard_map/ppermute | solution.py:646
  327.6 14.7 %collective-permute-start.11 = (bf16[3,48,2304]{2,1,0:T(8,128)(2,1)S(1)}, bf16[3,48,2304]{2,1,0:T(8,128)(2,1)S(1)}, u32[]{:S(2)}, u32[]{:S(2)}) collective-permute-start(bf16[3,48,2304]{2,1,0:T(8,128)(2,1)S(1)} %collective-permute-done.10.refs_2_), channel_id=1, source_target_pairs={{0,14},{1,15},{2,0},{3,1},{4,2},{5,3},{6,4},{7,5},{8,6},{9,7},{10,... | collective-permute-start | bytes 1990664 | tf_op jit(solution)/shard_map/ppermute | solution.py:645
  331.0 14.7 %collective-permute-start.3 = (bf16[3,48,2304]{2,1,0:T(8,128)(2,1)S(1)}, bf16[3,48,2304]{2,1,0:T(8,128)(2,1)S(1)}, u32[]{:S(2)}, u32[]{:S(2)}) collective-permute-start(bf16[3,48,2304]{2,1,0:T(8,128)(2,1)S(1)} %collective-permute-done.2.refs_0_), channel_id=1, source_target_pairs={{0,2},{1,3},{2,4},{3,5},{4,6},{5,7},{6,8},{7,9},{8,10},{9,11},{10,... | collective-permute-start | bytes 1990664 | tf_op jit(solution)/shard_map/ppermute | solution.py:644
  331.0 14.7 %collective-permute-start.27 = (bf16[3,48,2304]{2,1,0:T(8,128)(2,1)S(1)}, bf16[3,48,2304]{2,1,0:T(8,128)(2,1)S(1)}, u32[]{:S(2)}, u32[]{:S(2)}) collective-permute-start(bf16[3,48,2304]{2,1,0:T(8,128)(2,1)S(1)} %collective-permute-done.8.refs_2_), channel_id=1, source_target_pairs={{0,1},{1,0},{2,3},{3,2},{4,5},{5,4},{6,7},{7,6},{8,9},{9,8},{10,11... | collective-permute-start | bytes 1990664 | tf_op jit(solution)/shard_map/ppermute | solution.py:646
  336.0 14.8 %collective-permute-start.26 = (bf16[3,48,2304]{2,1,0:T(8,128)(2,1)S(1)}, bf16[3,48,2304]{2,1,0:T(8,128)(2,1)S(1)}, u32[]{:S(2)}, u32[]{:S(2)}) collective-permute-start(bf16[3,48,2304]{2,1,0:T(8,128)(2,1)S(1)} %collective-permute-done.refs_0_), channel_id=1, source_target_pairs={{0,1},{1,0},{2,3},{3,2},{4,5},{5,4},{6,7},{7,6},{8,9},{9,8},{10,11... | collective-permute-start | bytes 1990664 | tf_op jit(solution)/shard_map/ppermute | solution.py:646
  337.7 14.8 %collective-permute-start.25 = (bf16[3,48,2304]{2,1,0:T(8,128)(2,1)S(1)}, bf16[3,48,2304]{2,1,0:T(8,128)(2,1)S(1)}, u32[]{:S(2)}, u32[]{:S(2)}) collective-permute-start(bf16[3,48,2304]{2,1,0:T(8,128)(2,1)S(1)} %collective-permute-done.9.refs_2_), channel_id=1, source_target_pairs={{0,1},{1,0},{2,3},{3,2},{4,5},{5,4},{6,7},{7,6},{8,9},{9,8},{10,11... | collective-permute-start | bytes 1990664 | tf_op jit(solution)/shard_map/ppermute | solution.py:646
  342.3 13.9 %collective-permute-start.12 = (bf16[3,48,2304]{2,1,0:T(8,128)(2,1)S(1)}, bf16[3,48,2304]{2,1,0:T(8,128)(2,1)S(1)}, u32[]{:S(2)}, u32[]{:S(2)}) collective-permute-start(bf16[3,48,2304]{2,1,0:T(8,128)(2,1)S(1)} %collective-permute-done.11.refs_2_), channel_id=1, source_target_pairs={{0,14},{1,15},{2,0},{3,1},{4,2},{5,3},{6,4},{7,5},{8,6},{9,7},{10,... | collective-permute-start | bytes 1990664 | tf_op jit(solution)/shard_map/ppermute | solution.py:645
  345.7 13.9 %collective-permute-start.4 = (bf16[3,48,2304]{2,1,0:T(8,128)(2,1)S(1)}, bf16[3,48,2304]{2,1,0:T(8,128)(2,1)}, u32[]{:S(2)}, u32[]{:S(2)}) collective-permute-start(bf16[3,48,2304]{2,1,0:T(8,128)(2,1)S(1)} %collective-permute-done.3.refs_0_), channel_id=1, source_target_pairs={{0,2},{1,3},{2,4},{3,5},{4,6},{5,7},{6,8},{7,9},{8,10},{9,11},{10,... | collective-permute-start | bytes 1990664 | tf_op jit(solution)/shard_map/ppermute | solution.py:644
  346.6 13.0 %collective-permute-start.24 = (bf16[3,48,2304]{2,1,0:T(8,128)(2,1)S(1)}, bf16[3,48,2304]{2,1,0:T(8,128)(2,1)S(1)}, u32[]{:S(2)}, u32[]{:S(2)}) collective-permute-start(bf16[3,48,2304]{2,1,0:T(8,128)(2,1)S(1)} %collective-permute-done.1.refs_0_), channel_id=1, source_target_pairs={{0,1},{1,0},{2,3},{3,2},{4,5},{5,4},{6,7},{7,6},{8,9},{9,8},{10,11... | collective-permute-start | bytes 1990664 | tf_op jit(solution)/shard_map/ppermute | solution.py:646
  351.6 14.2 %collective-permute-start.23 = (bf16[3,48,2304]{2,1,0:T(8,128)(2,1)S(1)}, bf16[3,48,2304]{2,1,0:T(8,128)(2,1)S(1)}, u32[]{:S(2)}, u32[]{:S(2)}) collective-permute-start(bf16[3,48,2304]{2,1,0:T(8,128)(2,1)S(1)} %collective-permute-done.10.refs_2_), channel_id=1, source_target_pairs={{0,1},{1,0},{2,3},{3,2},{4,5},{5,4},{6,7},{7,6},{8,9},{9,8},{10,11... | collective-permute-start | bytes 1990664 | tf_op jit(solution)/shard_map/ppermute | solution.py:646
  353.3 13.4 %collective-permute-start.22 = (bf16[3,48,2304]{2,1,0:T(8,128)(2,1)S(1)}, bf16[3,48,2304]{2,1,0:T(8,128)(2,1)S(1)}, u32[]{:S(2)}, u32[]{:S(2)}) collective-permute-start(bf16[3,48,2304]{2,1,0:T(8,128)(2,1)S(1)} %collective-permute-done.2.refs_0_), channel_id=1, source_target_pairs={{0,1},{1,0},{2,3},{3,2},{4,5},{5,4},{6,7},{7,6},{8,9},{9,8},{10,11... | collective-permute-start | bytes 1990664 | tf_op jit(solution)/shard_map/ppermute | solution.py:646
  356.2 13.4 %collective-permute-start.13 = (bf16[3,48,2304]{2,1,0:T(8,128)(2,1)S(1)}, bf16[3,48,2304]{2,1,0:T(8,128)(2,1)}, u32[]{:S(2)}, u32[]{:S(2)}) collective-permute-start(bf16[3,48,2304]{2,1,0:T(8,128)(2,1)S(1)} %collective-permute-done.12.refs_2_), channel_id=1, source_target_pairs={{0,14},{1,15},{2,0},{3,1},{4,2},{5,3},{6,4},{7,5},{8,6},{9,7},{10,... | collective-permute-start | bytes 1990664 | tf_op jit(solution)/shard_map/ppermute | solution.py:645
  359.6 13.5 %collective-permute-start.5 = (bf16[3,48,2304]{2,1,0:T(8,128)(2,1)}, bf16[3,48,2304]{2,1,0:T(8,128)(2,1)}, u32[]{:S(2)}, u32[]{:S(2)}) collective-permute-start(bf16[3,48,2304]{2,1,0:T(8,128)(2,1)} %collective-permute-done.4.refs_0_), channel_id=1, source_target_pairs={{0,2},{1,3},{2,4},{3,5},{4,6},{5,7},{6,8},{7,9},{8,10},{9,11},{10,... | collective-permute-start | bytes 1990664 | tf_op jit(solution)/shard_map/ppermute | solution.py:644
  360.5 15.0 %collective-permute-start.21 = (bf16[3,48,2304]{2,1,0:T(8,128)(2,1)S(1)}, bf16[3,48,2304]{2,1,0:T(8,128)(2,1)}, u32[]{:S(2)}, u32[]{:S(2)}) collective-permute-start(bf16[3,48,2304]{2,1,0:T(8,128)(2,1)S(1)} %collective-permute-done.11.refs_2_), channel_id=1, source_target_pairs={{0,1},{1,0},{2,3},{3,2},{4,5},{5,4},{6,7},{7,6},{8,9},{9,8},{10,11... | collective-permute-start | bytes 1990664 | tf_op jit(solution)/shard_map/ppermute | solution.py:646
  366.7 15.6 %collective-permute-start.20 = (bf16[3,48,2304]{2,1,0:T(8,128)(2,1)S(1)}, bf16[3,48,2304]{2,1,0:T(8,128)(2,1)}, u32[]{:S(2)}, u32[]{:S(2)}) collective-permute-start(bf16[3,48,2304]{2,1,0:T(8,128)(2,1)S(1)} %collective-permute-done.3.refs_0_), channel_id=1, source_target_pairs={{0,1},{1,0},{2,3},{3,2},{4,5},{5,4},{6,7},{7,6},{8,9},{9,8},{10,11... | collective-permute-start | bytes 1990664 | tf_op jit(solution)/shard_map/ppermute | solution.py:646
  367.5 14.9 %collective-permute-start.19 = (bf16[3,48,2304]{2,1,0:T(8,128)(2,1)S(1)}, bf16[3,48,2304]{2,1,0:T(8,128)(2,1)}, u32[]{:S(2)}, u32[]{:S(2)}) collective-permute-start(bf16[3,48,2304]{2,1,0:T(8,128)(2,1)S(1)} %collective-permute-done.12.refs_2_), channel_id=1, source_target_pairs={{0,1},{1,0},{2,3},{3,2},{4,5},{5,4},{6,7},{7,6},{8,9},{9,8},{10,11... | collective-permute-start | bytes 1990664 | tf_op jit(solution)/shard_map/ppermute | solution.py:646
  369.5 13.5 %collective-permute-start.14 = (bf16[3,48,2304]{2,1,0:T(8,128)(2,1)}, bf16[3,48,2304]{2,1,0:T(8,128)(2,1)}, u32[]{:S(2)}, u32[]{:S(2)}) collective-permute-start(bf16[3,48,2304]{2,1,0:T(8,128)(2,1)} %collective-permute-done.13.refs_2_), channel_id=1, source_target_pairs={{0,14},{1,15},{2,0},{3,1},{4,2},{5,3},{6,4},{7,5},{8,6},{9,7},{10,... | collective-permute-start | bytes 1990664 | tf_op jit(solution)/shard_map/ppermute | solution.py:645
  373.1 16.3 %collective-permute-start.6 = (bf16[3,48,2304]{2,1,0:T(8,128)(2,1)}, bf16[3,48,2304]{2,1,0:T(8,128)(2,1)}, u32[]{:S(2)}, u32[]{:S(2)}) collective-permute-start(bf16[3,48,2304]{2,1,0:T(8,128)(2,1)} %collective-permute-done.5.refs_0_), channel_id=1, source_target_pairs={{0,2},{1,3},{2,4},{3,5},{4,6},{5,7},{6,8},{7,9},{8,10},{9,11},{10,... | collective-permute-start | bytes 1990664 | tf_op jit(solution)/shard_map/ppermute | solution.py:644
  375.5 82.0 %collective-permute-start.18 = (bf16[3,48,2304]{2,1,0:T(8,128)(2,1)}, bf16[3,48,2304]{2,1,0:T(8,128)(2,1)}, u32[]{:S(2)}, u32[]{:S(2)}) collective-permute-start(bf16[3,48,2304]{2,1,0:T(8,128)(2,1)} %collective-permute-done.4.refs_0_), channel_id=1, source_target_pairs={{0,1},{1,0},{2,3},{3,2},{4,5},{5,4},{6,7},{7,6},{8,9},{9,8},{10,11... | collective-permute-start | bytes 1990664 | tf_op jit(solution)/shard_map/ppermute | solution.py:646
  382.3 87.7 %collective-permute-start.17 = (bf16[3,48,2304]{2,1,0:T(8,128)(2,1)}, bf16[3,48,2304]{2,1,0:T(8,128)(2,1)}, u32[]{:S(2)}, u32[]{:S(2)}) collective-permute-start(bf16[3,48,2304]{2,1,0:T(8,128)(2,1)} %collective-permute-done.13.refs_2_), channel_id=1, source_target_pairs={{0,1},{1,0},{2,3},{3,2},{4,5},{5,4},{6,7},{7,6},{8,9},{9,8},{10,11... | collective-permute-start | bytes 1990664 | tf_op jit(solution)/shard_map/ppermute | solution.py:646
  382.5 87.5 %collective-permute-start.16 = (bf16[3,48,2304]{2,1,0:T(8,128)(2,1)}, bf16[3,48,2304]{2,1,0:T(8,128)(2,1)}, u32[]{:S(2)}, u32[]{:S(2)}) collective-permute-start(bf16[3,48,2304]{2,1,0:T(8,128)(2,1)} %collective-permute-done.5.refs_0_), channel_id=1, source_target_pairs={{0,1},{1,0},{2,3},{3,2},{4,5},{5,4},{6,7},{7,6},{8,9},{9,8},{10,11... | collective-permute-start | bytes 1990664 | tf_op jit(solution)/shard_map/ppermute | solution.py:646
  383.0 99.7 %collective-permute-start.15 = (bf16[3,48,2304]{2,1,0:T(8,128)(2,1)}, bf16[3,48,2304]{2,1,0:T(8,128)(2,1)}, u32[]{:S(2)}, u32[]{:S(2)}) collective-permute-start(bf16[3,48,2304]{2,1,0:T(8,128)(2,1)} %collective-permute-done.14.refs_2_), channel_id=1, source_target_pairs={{0,1},{1,0},{2,3},{3,2},{4,5},{5,4},{6,7},{7,6},{8,9},{9,8},{10,11... | collective-permute-start | bytes 1990664 | tf_op jit(solution)/shard_map/ppermute | solution.py:646
  389.4 93.3 %collective-permute-start.7 = (bf16[3,48,2304]{2,1,0:T(8,128)(2,1)}, bf16[3,48,2304]{2,1,0:T(8,128)(2,1)}, u32[]{:S(2)}, u32[]{:S(2)}) collective-permute-start(bf16[3,48,2304]{2,1,0:T(8,128)(2,1)} %collective-permute-done.6.refs_0_), channel_id=1, source_target_pairs={{0,1},{1,0},{2,3},{3,2},{4,5},{5,4},{6,7},{7,6},{8,9},{9,8},{10,11... | collective-permute-start | bytes 1990664 | tf_op jit(solution)/shard_map/ppermute | solution.py:646
  (26 other events, 132.7 us)
